TPU v7x, 512 devices: a whole 4x8x8 slice. The times are simulated.
512 devices in a mesh: gz: 32 (over z, x_lo, core), grp: 16 (over y, x_hi).
Axes of the slice: x: 4 (x_hi: 2, x_lo: 2; x = x_hi * 2 + x_lo), y: 8, z: 8, core: 2. Of those that a mesh axis runs over, the one named last changes fastest.
Arguments:
- volumes: bfloat16 [16, 64, 16, 1024], P('grp', 'gz'), may hold values from -6 to 6
- cotangent: bfloat16 [16, 32, 64, 128], P(None, 'gz', None, 'grp'), may hold values from -6 to 6
- fine_kernel: bfloat16 [1728, 64], replicated, may hold values from -0.15625 to 0.15625
- down_kernel: bfloat16 [512, 128], replicated, may hold values from -0.25 to 0.25
- coarse_kernel: bfloat16 [3456, 128], P(None, 'grp'), may hold values from -0.109375 to 0.109375
Outputs:
- coarse_out: bfloat16 [16, 32, 64, 128], P(None, 'gz', None, 'grp')
- volume_grad: bfloat16 [16, 64, 16, 1024], P('grp', 'gz')
- fine_kernel_grad: float32 [1728, 64], replicated
- down_kernel_grad: float32 [512, 128], replicated
- coarse_kernel_grad: float32 [3456, 128], P(None, 'grp')
All inputs are finite; a program needn't handle non-finite values.
Results may differ from a plain program's by a relative error of at most 0.019.
Values may be sent and summed in bfloat16 or wider, within the bound.
No kernel may reach another device: no remote copies, remote signals or barrier semaphores. Data moves between devices by JAX's collectives and lax.ppermute only.
A program may use at most 64 MiB of HBM per device.

v0:
```python
import jax
import jax.numpy as jnp
from jax import lax
from jax.sharding import PartitionSpec as P


def with_halo(array, sides, width):
    for axis, dim in sides:
        devices, length = (lax.axis_size(axis), array.shape[dim])
        up = [(i, (i + 1) % devices) for i in range(devices - 1)]
        down = [(j, i) for i, j in up]
        last = lax.slice_in_dim(array, length - width, length, axis=dim)
        initial = lax.slice_in_dim(array, 0, width, axis=dim)
        before = lax.ppermute(last, axis, up)
        after = lax.ppermute(initial, axis, down)
        array = jnp.concatenate([before, array, after], axis=dim)
    return array


def total_of_pieces(array, axis):
    parts = lax.all_gather(array, axis).astype(jnp.float32)
    return parts.sum(axis=0)


def in_order(parts, dim):
    dims = list(parts.shape[1:])
    dims[dim] *= parts.shape[0]
    return jnp.moveaxis(parts, 0, dim).reshape(dims)


def from_everyone(array, axis):
    devices = lax.axis_size(axis)
    return lax.all_to_all(
        jnp.broadcast_to(array[None], (devices, *array.shape)), axis, 0, 0, tiled=True
    )


def gathered_copies(array, axis, dim):
    return in_order(from_everyone(array, axis), dim)


def in_blocks(array, dim, devices):
    before, after = (array.shape[:dim], array.shape[dim + 1 :])
    return jnp.moveaxis(array.reshape(*before, devices, -1, *after), dim, 0)


def summed_on_arrival(array, axis, dim):
    devices = lax.axis_size(axis)
    parts = lax.all_to_all(in_blocks(array, dim, devices), axis, 0, 0, tiled=True)
    return jnp.sum(parts.astype(jnp.float32), axis=0)


def pad_sides(block):
    return jnp.pad(block, ((0, 0), (0, 0), (1, 1), (1, 1), (0, 0)))


def convolve(padded, kernel):
    samples, extent_z, extent_x, extent_y, channels = padded.shape
    extent_z, extent_x, extent_y = (extent_z - 2, extent_x - 2, extent_y - 2)
    summed = None
    for plane in range(3):
        pieces = [
            padded[
                :,
                plane : plane + extent_z,
                row_step : row_step + extent_x,
                col_step : col_step + extent_y,
                :,
            ]
            for row_step in range(3)
            for col_step in range(3)
        ]
        columns = jnp.concatenate(pieces, axis=-1).reshape(-1, 9 * channels)
        rows = kernel[plane * 9 * channels : (plane + 1) * 9 * channels]
        partial_value = jnp.dot(columns, rows, preferred_element_type=jnp.float32)
        summed = partial_value if summed is None else summed + partial_value
    return summed.reshape(samples, extent_z, extent_x, extent_y, -1)


def kernel_gradient(padded, grad):
    samples, extent_z, extent_x, extent_y, channels = padded.shape
    extent_z, extent_x, extent_y = (extent_z - 2, extent_x - 2, extent_y - 2)
    flat_grad = grad.reshape(-1, grad.shape[-1])
    blocks = []
    for plane in range(3):
        pieces = [
            padded[
                :,
                plane : plane + extent_z,
                row_step : row_step + extent_x,
                col_step : col_step + extent_y,
                :,
            ]
            for row_step in range(3)
            for col_step in range(3)
        ]
        columns = jnp.concatenate(pieces, axis=-1).reshape(-1, 9 * channels)
        blocks.append(
            lax.dot_general(
                columns, flat_grad, (((0,), (0,)), ((), ())), preferred_element_type=jnp.float32
            )
        )
    return jnp.concatenate(blocks, axis=0)


def flip_kernel(kernel, inputs):
    outputs = kernel.shape[1]
    shaped = kernel.reshape(3, 3, 3, inputs, outputs)[::-1, ::-1, ::-1]
    return jnp.transpose(shaped, (0, 1, 2, 4, 3)).reshape(27 * outputs, inputs)


def silu_slope(value):
    sigmoid_v = jax.nn.sigmoid(value)
    return sigmoid_v * (1.0 + value * (1.0 - sigmoid_v))


def pool_columns(block):
    samples, extent_z, extent_x, extent_y, channels = block.shape
    shaped = block.reshape(samples, extent_z // 2, 2, extent_x // 2, 2, extent_y // 2, 2, channels)
    return jnp.transpose(shaped, (0, 1, 3, 5, 2, 4, 6, 7)).reshape(-1, 8 * channels)


def unpool_columns(flat, samples, extent_z, extent_x, extent_y, channels):
    shaped = flat.reshape(samples, extent_z // 2, extent_x // 2, extent_y // 2, 2, 2, 2, channels)
    return jnp.transpose(shaped, (0, 1, 4, 2, 5, 3, 6, 7)).reshape(
        samples, extent_z, extent_x, extent_y, channels
    )


def coarse_rim(block):
    return with_halo(block, (("gz", 1),), 1)


def coarse_grad_rim(block):
    return with_halo(block, (("gz", 1),), 1)


def coarse_kernel_total(partial_value):
    return total_of_pieces(partial_value.astype(jnp.bfloat16), "gz").astype(jnp.float32)


def per_device(volumes, cotangent, fine_kernel, down_kernel, coarse_kernel):
    samples, planes, xfine, packed = volumes.shape
    cfine = fine_kernel.shape[1]
    yfine = packed // cfine
    fine = volumes.reshape(samples, planes, xfine, yfine, cfine)
    fine_padded = pad_sides(with_halo(fine, (("gz", 1),), 1))
    fine_pre = convolve(fine_padded, fine_kernel)
    fine_act = jax.nn.silu(fine_pre).astype(jnp.bfloat16)
    pooled = pool_columns(fine_act)
    coarse_in = jnp.dot(pooled, down_kernel, preferred_element_type=jnp.float32).astype(
        jnp.bfloat16
    )
    coarse_in = coarse_in.reshape(samples, planes // 2, xfine // 2, yfine // 2, -1)
    coarse_framed = coarse_rim(coarse_in)
    full_kernel = gathered_copies(coarse_kernel, "grp", 1)
    own_padded = pad_sides(coarse_framed)
    coarse_pre = convolve(own_padded, full_kernel)
    group, zcoarse, xcoarse, ycoarse, all_channels = coarse_pre.shape
    own_out = (
        jax.nn.silu(coarse_pre)
        .astype(jnp.bfloat16)
        .reshape(group, zcoarse, xcoarse * ycoarse, all_channels)
    )
    coarse_out = lax.all_to_all(own_out, "grp", split_axis=3, concat_axis=0, tiled=True)
    grad_own = lax.all_to_all(cotangent, "grp", split_axis=0, concat_axis=3, tiled=True)
    grad_shaped = grad_own.reshape(coarse_pre.shape).astype(jnp.float32)
    coarse_grad = (grad_shaped * silu_slope(coarse_pre)).astype(jnp.bfloat16)
    whole_kg = kernel_gradient(own_padded, coarse_grad)
    coarse_kg = coarse_kernel_total(summed_on_arrival(whole_kg.astype(jnp.bfloat16), "grp", 1))
    partial_value = convolve(
        pad_sides(coarse_grad_rim(coarse_grad)), flip_kernel(full_kernel, all_channels)
    )
    coarse_in_grad = partial_value.astype(jnp.bfloat16)
    flat_in_grad = coarse_in_grad.reshape(-1, coarse_in_grad.shape[-1])
    pooled_grad = jnp.dot(flat_in_grad, down_kernel.T, preferred_element_type=jnp.float32)
    fine_act_grad = unpool_columns(pooled_grad, samples, planes, xfine, yfine, cfine)
    down_kg = lax.dot_general(
        pooled, flat_in_grad, (((0,), (0,)), ((), ())), preferred_element_type=jnp.float32
    )
    fine_grad = (fine_act_grad * silu_slope(fine_pre)).astype(jnp.bfloat16)
    fine_kg = kernel_gradient(fine_padded, fine_grad)
    fine_kg, down_kg = lax.psum((fine_kg, down_kg), ("gz", "grp"))
    grad_padded = pad_sides(with_halo(fine_grad, (("gz", 1),), 1))
    volume_grad = convolve(grad_padded, flip_kernel(fine_kernel, cfine)).astype(jnp.bfloat16)
    volume_grad = volume_grad.reshape(samples, planes, xfine, packed)
    return (coarse_out, volume_grad, fine_kg, down_kg, coarse_kg)


def solution(mesh):
    in_specs = (P("grp", "gz", None, None), P(None, "gz", None, "grp"), P(), P(), P(None, "grp"))
    out_specs = (P(None, "gz", None, "grp"), P("grp", "gz", None, None), P(), P(), P(None, "grp"))
    return jax.shard_map(
        per_device, mesh=mesh, in_specs=in_specs, out_specs=out_specs, check_vma=False
    )
```

profile of v0, /device:TPU:1, one launch (start us, length us, event | category | flops | bytes accessed | tf_op | source)
XLA Modules:
  0.0 436.0 jit_solution(9126026239586204681)
XLA Ops:
  9.1 4.5 %collective-permute-start = (bf16[1,1,16,16,64]{4,3,2,1,0:T(8,128)(2,1)S(1)}, bf16[1,1,16,16,64]{4,3,2,1,0:T(8,128)(2,1)S(1)}, u32[]{:S(2)}, u32[]{:S(2)}) collective-permute-start(bf16[1,1,16,16,64]{4,3,2,1,0:T(8,128)(2,1)S(1)} %get-tuple-element.77), channel_id=1, source_target_pairs={{0,16},{16,32},{32,48},{48,64},{64,80},{80,96},{96,112},{112,128},... | collective-permute-start | bytes 98312 | tf_op jit(solution)/shard_map/ppermute | solution.py:14
  13.6 5.5 %collective-permute-start.1 = (bf16[1,1,16,16,64]{4,3,2,1,0:T(8,128)(2,1)S(1)}, bf16[1,1,16,16,64]{4,3,2,1,0:T(8,128)(2,1)S(1)}, u32[]{:S(2)}, u32[]{:S(2)}) collective-permute-start(bf16[1,1,16,16,64]{4,3,2,1,0:T(8,128)(2,1)S(1)} %get-tuple-element.78), channel_id=1, source_target_pairs={{16,0},{32,16},{48,32},{64,48},{80,64},{96,80},{112,96},{128,112},... | collective-permute-start | bytes 98312 | tf_op jit(solution)/shard_map/ppermute | solution.py:15
  19.1 1.5 reshape.461
  20.6 5.5 %all-to-all-start.2 = ((bf16[16,2,256]{2,1,0:T(2,128)(2,1)}), bf16[16,2,256]{2,1,0:T(2,128)(2,1)S(1)}, u32[]{:S(2)}, u32[]{:S(2)}) async-start(bf16[16,2,256]{2,1,0:T(2,128)(2,1)} %reshape.461), calls=%async_computation.2 | async-start | bytes 32768 | tf_op jit(solution)/shard_map/all_to_all | solution.py:166
  26.1 1.5 reshape.428
  27.6 1.7 rev.7
  31.8 3.2 all-to-all-done.2
  36.0 5.9 %all-to-all-start = ((bf16[16,3456,8]{1,2,0:T(8,128)(2,1)}), bf16[16,3456,8]{1,2,0:T(8,128)(2,1)S(1)}, u32[]{:S(2)}, u32[]{:S(2)}) async-start(bf16[16,3456,8]{1,2,0:T(8,128)(2,1)} %broadcast_in_dim.2), calls=%async_computation | async-start | bytes 1769472 | tf_op jit(solution)/shard_map/all_to_all | solution.py:33
  44.6 1.9 fusion.27
  46.4 1.6 pad_maximum_fusion.2
  48.1 1.4 concatenate.150
  49.6 1.9 convolution_add_fusion.3
  54.8 3.9 collective-permute-start.2
  58.7 1.9 collective-permute-start.3
  63.9 1.8 copy.94
  66.6 1.5 copy.59
  68.1 2.1 concatenate.201
  75.5 3.6 collective-permute-start.4
  79.2 1.9 collective-permute-start.5
  83.7 9.9 %all-to-all-start.3 = ((bf16[16,3456,8]{1,2,0:T(8,128)(2,1)}), bf16[16,3456,8]{1,2,0:T(8,128)(2,1)S(1)}, u32[]{:S(2)}, u32[]{:S(2)}) async-start(bf16[16,3456,8]{1,2,0:T(8,128)(2,1)} %copy.84), calls=%async_computation.3 | async-start | bytes 1769472 | tf_op jit(solution)/shard_map/all_to_all | solution.py:49
  93.6 5.8 %rev.6 = bf16[3,3,3,128,128]{3,2,1,0,4:T(4,128)(2,1)S(1)} reverse(bf16[3,3,3,128,128]{3,2,1,0,4:T(4,128)(2,1)} %reshape_reshape.3), dimensions={0,1,2} | reverse | bytes 1769472 | tf_op jit(solution)/shard_map/rev | solution.py:108
  109.5 10.6 %all-to-all-done.3 = bf16[16,3456,8]{1,2,0:T(8,128)(2,1)S(1)} async-done(((bf16[16,3456,8]{1,2,0:T(8,128)(2,1)}), bf16[16,3456,8]{1,2,0:T(8,128)(2,1)S(1)}, u32[]{:S(2)}, u32[]{:S(2)}) %all-to-all-start.3) | async-done | bytes 884768 | tf_op jit(solution)/shard_map/all_to_all | solution.py:49
  120.2 3.5 all-to-all-start.1
  131.4 4.2 collective-permute-start.6
  135.7 2.1 collective-permute-start.7
  145.5 1.6 copy.68
  147.1 1.6 copy.69
  160.9 41.3 %all-gather.3.cloned.1.call-done = bf16[110592,8]{0,1:T(8,128)(2,1)} async-done(((bf16[3456,8]{0,1:T(8,128)(2,1)}), bf16[110592,8]{0,1:T(8,128)(2,1)}) %all-gather.3.cloned.1.call-update) | async-done | bytes 1769488 | tf_op jit(solution)/shard_map/all_gather | solution.py:21
  202.2 2.4 convert_reduce_fusion
  204.6 220.4 %all-reduce.7.cloned.1.call-done = (f32[1728,64]{0,1:T(8,128)}, f32[512,128]{1,0:T(8,128)}) async-done(((f32[1728,64]{0,1:T(8,128)}, f32[512,128]{1,0:T(8,128)}), (f32[1728,64]{0,1:T(8,128)}, f32[512,128]{1,0:T(8,128)})) %all-reduce.7.cloned.1.call-update) | async-done | bytes 704528 | tf_op jit(solution)/shard_map/psum | solution.py:183
  425.0 1.8 copy.170
  426.8 1.7 copy.171
  (213 shorter events, 59.4 us)
Async XLA Ops:
  8.0 46.6 %copy-start = (bf16[512,128]{1,0:T(8,128)(2,1)S(1)}, bf16[512,128]{1,0:T(8,128)(2,1)}, u32[]{:S(2)}) copy-start(bf16[512,128]{1,0:T(8,128)(2,1)} %param.8) | copy-start | bytes 393220
  9.1 20.5 %copy-start.24 = (bf16[1,2,16,1024]{3,2,1,0:T(8,128)(2,1)S(1)}, bf16[1,2,16,1024]{3,2,1,0:T(8,128)(2,1)}, u32[]{:S(2)}) copy-start(bf16[1,2,16,1024]{3,2,1,0:T(8,128)(2,1)} %param.5) | copy-start | bytes 196612
  9.1 32.8 %collective-permute-start = (bf16[1,1,16,16,64]{4,3,2,1,0:T(8,128)(2,1)S(1)}, bf16[1,1,16,16,64]{4,3,2,1,0:T(8,128)(2,1)S(1)}, u32[]{:S(2)}, u32[]{:S(2)}) collective-permute-start(bf16[1,1,16,16,64]{4,3,2,1,0:T(8,128)(2,1)S(1)} %get-tuple-element.77), channel_id=1, source_target_pairs={{0,16},{16,32},{32,48},{48,64},{64,80},{80,96},{96,112},{112,128},... | collective-permute-start | bytes 98312 | tf_op jit(solution)/shard_map/ppermute | solution.py:14
  13.6 28.4 %collective-permute-start.1 = (bf16[1,1,16,16,64]{4,3,2,1,0:T(8,128)(2,1)S(1)}, bf16[1,1,16,16,64]{4,3,2,1,0:T(8,128)(2,1)S(1)}, u32[]{:S(2)}, u32[]{:S(2)}) collective-permute-start(bf16[1,1,16,16,64]{4,3,2,1,0:T(8,128)(2,1)S(1)} %get-tuple-element.78), channel_id=1, source_target_pairs={{16,0},{32,16},{48,32},{64,48},{80,64},{96,80},{112,96},{128,112},... | collective-permute-start | bytes 98312 | tf_op jit(solution)/shard_map/ppermute | solution.py:15
  20.6 14.4 %all-to-all-start.2 = ((bf16[16,2,256]{2,1,0:T(2,128)(2,1)}), bf16[16,2,256]{2,1,0:T(2,128)(2,1)S(1)}, u32[]{:S(2)}, u32[]{:S(2)}) async-start(bf16[16,2,256]{2,1,0:T(2,128)(2,1)} %reshape.461), calls=%async_computation.2 | async-start | bytes 32768 | tf_op jit(solution)/shard_map/all_to_all | solution.py:166
  27.6 7.4 %copy-start.33 = (bf16[3456,8]{0,1:T(8,128)(2,1)S(1)}, bf16[3456,8]{0,1:T(8,128)(2,1)}, u32[]{:S(2)}) copy-start(bf16[3456,8]{0,1:T(8,128)(2,1)} %param.9) | copy-start | bytes 165892
  36.0 36.9 %all-to-all-start = ((bf16[16,3456,8]{1,2,0:T(8,128)(2,1)}), bf16[16,3456,8]{1,2,0:T(8,128)(2,1)S(1)}, u32[]{:S(2)}, u32[]{:S(2)}) async-start(bf16[16,3456,8]{1,2,0:T(8,128)(2,1)} %broadcast_in_dim.2), calls=%async_computation | async-start | bytes 1769472 | tf_op jit(solution)/shard_map/all_to_all | solution.py:33
  44.0 4.1 copy-start.6
  44.0 4.1 copy-start.4
  44.0 8.8 %copy-start.5 = (bf16[1,2,16,16,64]{4,3,2,1,0:T(8,128)(2,1)}, bf16[1,2,16,16,64]{4,3,2,1,0:T(8,128)(2,1)S(1)}, u32[]{:S(2)}) copy-start(bf16[1,2,16,16,64]{4,3,2,1,0:T(8,128)(2,1)S(1)} %get-tuple-element.58) | copy-start | bytes 196612
  54.1 7.2 %copy-start.10 = (f32[512,64]{0,1:T(8,128)}, f32[512,64]{0,1:T(8,128)S(1)}, u32[]{:S(2)}) copy-start(f32[512,64]{0,1:T(8,128)S(1)} %convolution_add_fusion.2) | copy-start | bytes 393220
  54.3 13.8 %copy-start.2 = (f32[512,64]{1,0:T(8,128)}, f32[512,64]{1,0:T(8,128)S(1)}, u32[]{:S(2)}) copy-start(f32[512,64]{1,0:T(8,128)S(1)} %copy.52) | copy-start | bytes 393220
  54.7 4.1 copy-start.13
  54.8 15.4 %collective-permute-start.2 = (bf16[1,1,8,8,128]{4,3,2,1,0:T(8,128)(2,1)S(1)}, bf16[1,1,8,8,128]{4,3,2,1,0:T(8,128)(2,1)}, u32[]{:S(2)}, u32[]{:S(2)}) collective-permute-start(bf16[1,1,8,8,128]{4,3,2,1,0:T(8,128)(2,1)S(1)} %bitcast.336), channel_id=1, source_target_pairs={{0,16},{16,32},{32,48},{48,64},{64,80},{80,96},{96,112},{112,128},... | collective-permute-start | bytes 49160 | tf_op jit(solution)/shard_map/ppermute | solution.py:14
  58.7 11.5 %collective-permute-start.3 = (bf16[1,1,8,8,128]{4,3,2,1,0:T(8,128)(2,1)S(1)}, bf16[1,1,8,8,128]{4,3,2,1,0:T(8,128)(2,1)}, u32[]{:S(2)}, u32[]{:S(2)}) collective-permute-start(bf16[1,1,8,8,128]{4,3,2,1,0:T(8,128)(2,1)S(1)} %bitcast.337), channel_id=1, source_target_pairs={{16,0},{32,16},{48,32},{64,48},{80,64},{96,80},{112,96},{128,112},... | collective-permute-start | bytes 49160 | tf_op jit(solution)/shard_map/ppermute | solution.py:15
  68.1 5.3 %copy-start.34 = (f32[1,1,8,8,128]{4,3,2,1,0:T(8,128)S(1)}, f32[1,1,8,8,128]{4,3,2,1,0:T(8,128)}, u32[]{:S(2)}) copy-start(f32[1,1,8,8,128]{4,3,2,1,0:T(8,128)} %copy.94) | copy-start | bytes 98308
  75.5 27.4 %collective-permute-start.4 = (bf16[1,1,8,8,128]{4,3,2,1,0:T(8,128)(2,1)}, bf16[1,1,8,8,128]{4,3,2,1,0:T(8,128)(2,1)}, u32[]{:S(2)}, u32[]{:S(2)}) collective-permute-start(bf16[1,1,8,8,128]{4,3,2,1,0:T(8,128)(2,1)} %get-tuple-element.120), channel_id=1, source_target_pairs={{0,16},{16,32},{32,48},{48,64},{64,80},{80,96},{96,112},{112,128},... | collective-permute-start | bytes 49160 | tf_op jit(solution)/shard_map/ppermute | solution.py:14
  79.2 23.8 %collective-permute-start.5 = (bf16[1,1,8,8,128]{4,3,2,1,0:T(8,128)(2,1)}, bf16[1,1,8,8,128]{4,3,2,1,0:T(8,128)(2,1)}, u32[]{:S(2)}, u32[]{:S(2)}) collective-permute-start(bf16[1,1,8,8,128]{4,3,2,1,0:T(8,128)(2,1)} %get-tuple-element.120), channel_id=1, source_target_pairs={{16,0},{32,16},{48,32},{64,48},{80,64},{96,80},{112,96},{128,112},... | collective-permute-start | bytes 49160 | tf_op jit(solution)/shard_map/ppermute | solution.py:15
  83.7 36.5 %all-to-all-start.3 = ((bf16[16,3456,8]{1,2,0:T(8,128)(2,1)}), bf16[16,3456,8]{1,2,0:T(8,128)(2,1)S(1)}, u32[]{:S(2)}, u32[]{:S(2)}) async-start(bf16[16,3456,8]{1,2,0:T(8,128)(2,1)} %copy.84), calls=%async_computation.3 | async-start | bytes 1769472 | tf_op jit(solution)/shard_map/all_to_all | solution.py:49
  99.9 7.9 %copy-start.31 = (f32[64,128]{1,0:T(8,128)S(1)}, f32[64,128]{1,0:T(8,128)}, u32[]{:S(2)}) copy-start(f32[64,128]{1,0:T(8,128)} %copy.59) | copy-start | bytes 98308
  103.7 27.0 %copy-start.3 = (f32[512,64]{1,0:T(8,128)S(1)}, f32[512,64]{1,0:T(8,128)}, u32[]{:S(2)}) copy-start(f32[512,64]{1,0:T(8,128)} %copy-done.2) | copy-start | bytes 393220
  104.6 4.4 %copy-start.30 = (bf16[1,1,8,8,1152]{4,3,2,1,0:T(8,128)(2,1)}, bf16[1,1,8,8,1152]{4,3,2,1,0:T(8,128)(2,1)S(1)}, u32[]{:S(2)}) copy-start(bf16[1,1,8,8,1152]{4,3,2,1,0:T(8,128)(2,1)S(1)} %constant_dynamic-update-slice_fusion.31) | copy-start | bytes 442372
  120.2 21.0 %all-to-all-start.1 = ((bf16[16,2,256]{2,1,0:T(2,128)(2,1)}), bf16[16,2,256]{2,1,0:T(2,128)(2,1)S(1)}, u32[]{:S(2)}, u32[]{:S(2)}) async-start(bf16[16,2,256]{2,1,0:T(2,128)(2,1)} %reshape.459), calls=%async_computation.1 | async-start | bytes 32768 | tf_op jit(solution)/shard_map/all_to_all | solution.py:165
  123.7 78.5 %all-gather.3.cloned.1.call-start = ((), (), s32[]{:S(2)}) async-start(), calls=%async_computation.4 | async-start | bytes 1824768 | tf_op jit(solution)/shard_map/all_gather | solution.py:21
  124.5 300.5 %all-reduce.7.cloned.1.call-start = ((), (), s32[]{:S(2)}) async-start(), calls=%async_computation.5 | async-start | bytes 1441792 | tf_op jit(solution)/shard_map/psum | solution.py:183
  131.0 7.3 %copy-start.14 = (bf16[64,512]{1,0:T(8,128)(2,1)S(1)}, bf16[64,512]{1,0:T(8,128)(2,1)}, u32[]{:S(2)}) copy-start(bf16[64,512]{1,0:T(8,128)(2,1)} %copy-done.13) | copy-start | bytes 196612
  131.1 8.1 %copy-start.1 = (bf16[1,2,16,16,576]{4,3,2,1,0:T(8,128)(2,1)S(1)}, bf16[1,2,16,16,576]{4,3,2,1,0:T(8,128)(2,1)}, u32[]{:S(2)}) copy-start(bf16[1,2,16,16,576]{4,3,2,1,0:T(8,128)(2,1)} %concatenate.201) | copy-start | bytes 1769476
  131.4 10.5 %collective-permute-start.6 = (bf16[1,1,16,16,64]{4,3,2,1,0:T(8,128)(2,1)S(1)}, bf16[1,1,16,16,64]{4,3,2,1,0:T(8,128)(2,1)S(1)}, u32[]{:S(2)}, u32[]{:S(2)}) collective-permute-start(bf16[1,1,16,16,64]{4,3,2,1,0:T(8,128)(2,1)S(1)} %get-tuple-element.73), channel_id=1, source_target_pairs={{0,16},{16,32},{32,48},{48,64},{64,80},{80,96},{96,112},{112,128},... | collective-permute-start | bytes 98312 | tf_op jit(solution)/shard_map/ppermute | solution.py:14
  135.7 6.3 %collective-permute-start.7 = (bf16[1,1,16,16,64]{4,3,2,1,0:T(8,128)(2,1)S(1)}, bf16[1,1,16,16,64]{4,3,2,1,0:T(8,128)(2,1)S(1)}, u32[]{:S(2)}, u32[]{:S(2)}) collective-permute-start(bf16[1,1,16,16,64]{4,3,2,1,0:T(8,128)(2,1)S(1)} %get-tuple-element.74), channel_id=1, source_target_pairs={{16,0},{32,16},{48,32},{64,48},{80,64},{96,80},{112,96},{128,112},... | collective-permute-start | bytes 98312 | tf_op jit(solution)/shard_map/ppermute | solution.py:15
  144.6 10.8 %copy-start.11 = (f32[512,64]{0,1:T(8,128)S(1)}, f32[512,64]{0,1:T(8,128)}, u32[]{:S(2)}) copy-start(f32[512,64]{0,1:T(8,128)} %copy-done.10) | copy-start | bytes 393220
  144.6 10.8 %copy-start.22 = (f32[512,64]{0,1:T(8,128)S(1)}, f32[512,64]{0,1:T(8,128)}, u32[]{:S(2)}) copy-start(f32[512,64]{0,1:T(8,128)} %copy.66) | copy-start | bytes 393220
  145.4 10.2 %copy-start.17 = (bf16[1,3,3,64,64]{4,3,2,1,0:T(8,128)(2,1)S(1)}, bf16[1,3,3,64,64]{4,3,2,1,0:T(8,128)(2,1)}, u32[]{:S(2)}) copy-start(bf16[1,3,3,64,64]{4,3,2,1,0:T(8,128)(2,1)} %copy.75) | copy-start | bytes 221188
  (17 other events, 43.3 us)
Sparse Core Ops, SparseCore 0:
  126.6 75.5 all-gather.2
Sparse Core Ops, SparseCore 1:
  141.3 283.7 all-reduce.6
where the time goes:
time: 438 us; the launch traced here: 436 us
  waiting for transfers between devices  276 us (63%)
  local copies, waits for them, and re-layouts  67.7 us (15%)
  starting transfers between devices  52.6 us (12%)
  between operations  16.5 us (4%)
  matrix products  13.5 us (3%)
  other arithmetic  10.1 us (2%)
    psum x1, waiting for transfers between devices, per_device(): fine_kg, down_kg = lax.psum((fine_kg, down_kg), ('gz', 'grp'))  220 us
    all_gather x1, waiting for transfers between devices, total_of_pieces(): parts = lax.all_gather(array, axis).astype(jnp.float32)  41.3 us
    unnamed x119, local copies, waits for them, and re-layouts  20.8 us
    concatenate x21, local copies, waits for them, and re-layouts, convolve(): columns = jnp.concatenate(pieces, axis=-1).reshape(-1, 9 * channels)  16.9 us
    ppermute x4, starting transfers between devices, with_halo(): before = lax.ppermute(last, axis, up)  16.3 us
    ppermute x4, starting transfers between devices, with_halo(): after = lax.ppermute(initial, axis, down)  11.5 us
    all_to_all x1, waiting for transfers between devices, summed_on_arrival(): lax.all_to_all(in_blocks(array, dim, devices), axis, 0, 0, tiled=True)  10.6 us
    dot_general x12, matrix products, convolve(): partial_value = jnp.dot(columns, rows, preferred_element_type=jnp.float32)  10.5 us
  transfers between devices with their start and end apart: 14, of which 4 were waited for; matrix products, arithmetic and copies ran while one was open for 19% of the time, Pallas kernels for 0%

commit v1 on v0

--- a/solution.py
+++ b/solution.py
@@ -17,11 +17,6 @@
     return array
 
 
-def total_of_pieces(array, axis):
-    parts = lax.all_gather(array, axis).astype(jnp.float32)
-    return parts.sum(axis=0)
-
-
 def in_order(parts, dim):
     dims = list(parts.shape[1:])
     dims[dim] *= parts.shape[0]
@@ -135,8 +130,35 @@
     return with_halo(block, (("gz", 1),), 1)
 
 
-def coarse_kernel_total(partial_value):
-    return total_of_pieces(partial_value.astype(jnp.bfloat16), "gz").astype(jnp.float32)
+def gathered(block, axis):
+    return from_everyone(block, axis)
+
+
+def total_over_slice(fine_kg, down_kg, coarse_kg):
+    half = fine_kg.shape[0] // 2
+    packed_fine = jnp.concatenate([fine_kg[:half], fine_kg[half:]], axis=1)
+    shared = jnp.concatenate([packed_fine, down_kg], axis=0)
+    local = coarse_kg.T.reshape(-1, 128)
+    slabs = lax.axis_size("gz")
+    rows = -(-shared.shape[0] // (8 * slabs)) * 8
+    own_rows = -(-local.shape[0] // (8 * slabs)) * 8
+    shared_blocks = jnp.pad(shared, ((0, rows * slabs - shared.shape[0]), (0, 0)))
+    local_blocks = jnp.pad(local, ((0, own_rows * slabs - local.shape[0]), (0, 0)))
+    blocks = jnp.concatenate(
+        [shared_blocks.reshape(slabs, rows, 128), local_blocks.reshape(slabs, own_rows, 128)], axis=1
+    ).astype(jnp.bfloat16)
+    arrived = lax.all_to_all(blocks, "gz", 0, 0, tiled=True).astype(jnp.float32).sum(axis=0)
+    arrived = arrived.astype(jnp.bfloat16)
+    everyone = gathered(arrived[:rows], "grp").astype(jnp.float32).sum(axis=0)
+    final = jnp.concatenate([everyone.astype(jnp.bfloat16), arrived[rows:]], axis=0)
+    final = gathered(final, "gz").astype(jnp.float32)
+    shared_final = final[:, :rows].reshape(-1, 128)
+    local_final = final[:, rows:].reshape(-1, 128)[: local.shape[0]]
+    fine_total = shared_final[:half]
+    fine_total = jnp.concatenate([fine_total[:, :64], fine_total[:, 64:]], axis=0)
+    down_total = shared_final[half : half + down_kg.shape[0]]
+    coarse_total = local_final.reshape(coarse_kg.shape[1], coarse_kg.shape[0]).T
+    return fine_total, down_total, coarse_total
 
 
 def per_device(volumes, cotangent, fine_kernel, down_kernel, coarse_kernel):
@@ -167,7 +189,7 @@
     grad_shaped = grad_own.reshape(coarse_pre.shape).astype(jnp.float32)
     coarse_grad = (grad_shaped * silu_slope(coarse_pre)).astype(jnp.bfloat16)
     whole_kg = kernel_gradient(own_padded, coarse_grad)
-    coarse_kg = coarse_kernel_total(summed_on_arrival(whole_kg.astype(jnp.bfloat16), "grp", 1))
+    coarse_kg = summed_on_arrival(whole_kg.astype(jnp.bfloat16), "grp", 1)
     partial_value = convolve(
         pad_sides(coarse_grad_rim(coarse_grad)), flip_kernel(full_kernel, all_channels)
     )
@@ -180,7 +202,7 @@
     )
     fine_grad = (fine_act_grad * silu_slope(fine_pre)).astype(jnp.bfloat16)
     fine_kg = kernel_gradient(fine_padded, fine_grad)
-    fine_kg, down_kg = lax.psum((fine_kg, down_kg), ("gz", "grp"))
+    fine_kg, down_kg, coarse_kg = total_over_slice(fine_kg, down_kg, coarse_kg)
     grad_padded = pad_sides(with_halo(fine_grad, (("gz", 1),), 1))
     volume_grad = convolve(grad_padded, flip_kernel(fine_kernel, cfine)).astype(jnp.bfloat16)
     volume_grad = volume_grad.reshape(samples, planes, xfine, packed)

time: 438 us -> 214 us (0.49)
  waiting for transfers between devices: 276 us -> 42.8 us
  starting transfers between devices: 52.6 us -> 79 us
  between operations: 16.5 us -> 1.86 us
    psum x1 -> x0, waiting for transfers between devices: 220 us -> none  [per_device(): fine_kg, down_kg = lax.psum((fine_kg, down_kg), ('gz', 'grp'))]
    all_gather x1 -> x0, waiting for transfers between devices: 41.3 us -> none  [total_of_pieces(): parts = lax.all_gather(array, axis).astype(jnp.float32)]
    all_to_all x1 -> x3, waiting for transfers between devices: 0.01 us -> 16.7 us  [from_everyone(): lax.all_to_all(jnp.broadcast_to(array[None], (devices, *array.shape)), ax...]
    all_to_all x0 -> x1, starting transfers between devices: none -> 15.5 us  [total_over_slice(): lax.all_to_all(blocks, 'gz', 0, 0, tiled=True).astype(jnp.float32)]
    all_to_all x1 -> x3, starting transfers between devices: 5.85 us -> 16.1 us  [from_everyone(): lax.all_to_all(jnp.broadcast_to(array[None], (devices, *array.shape)), ax...]
    all_to_all x1, starting transfers between devices: 3.5 us -> 9.95 us  [per_device(): lax.all_to_all(own_out, 'grp', split_axis=3, concat_axis=0, tiled=True)]
    all_to_all x1, starting transfers between devices: 9.94 us -> 4.42 us  [summed_on_arrival(): lax.all_to_all(in_blocks(array, dim, devices), axis, 0, 0, tiled=True)]
    all_to_all x0 -> x1, waiting for transfers between devices: none -> 4.74 us  [total_over_slice(): lax.all_to_all(blocks, 'gz', 0, 0, tiled=True).astype(jnp.float32)]
  transfers between devices with their start and end apart: 14 -> 15, of which waited for: 4 -> 7; matrix products, arithmetic and copies ran while one was open for 19% -> 36% of each run, Pallas kernels for 0% -> 0%
where the time goes in v1:
time: 214 us; the launch traced here: 212 us
  starting transfers between devices  79 us (37%)
  local copies, waits for them, and re-layouts  64 us (30%)
  waiting for transfers between devices  42.8 us (20%)
  matrix products  14.9 us (7%)
  other arithmetic  9.44 us (4%)
    unnamed x131, local copies, waits for them, and re-layouts  18 us
    all_to_all x3, waiting for transfers between devices, from_everyone(): lax.all_to_all(jnp.broadcast_to(array[None], (devices, *array.shape)), ax...  16.7 us
    all_to_all x3, starting transfers between devices, from_everyone(): lax.all_to_all(jnp.broadcast_to(array[None], (devices, *array.shape)), ax...  16.1 us
    ppermute x4, starting transfers between devices, with_halo(): before = lax.ppermute(last, axis, up)  16 us
    all_to_all x1, starting transfers between devices, total_over_slice(): lax.all_to_all(blocks, 'gz', 0, 0, tiled=True).astype(jnp.float32)  15.5 us
    concatenate x21, local copies, waits for them, and re-layouts, convolve(): columns = jnp.concatenate(pieces, axis=-1).reshape(-1, 9 * channels)  14.9 us
    all_to_all x1, waiting for transfers between devices, summed_on_arrival(): lax.all_to_all(in_blocks(array, dim, devices), axis, 0, 0, tiled=True)  12.2 us
    ppermute x4, starting transfers between devices, with_halo(): after = lax.ppermute(initial, axis, down)  11.5 us
  transfers between devices with their start and end apart: 15, of which 7 were waited for; matrix products, arithmetic and copies ran while one was open for 36% of the time, Pallas kernels for 0%

profile of v1, /device:TPU:1, one launch (start us, length us, event | category | flops | bytes accessed | tf_op | source)
XLA Modules:
  0.0 211.9 jit_solution(18102704386527236433)
XLA Ops:
  1.7 4.5 %collective-permute-start = (bf16[1,1,16,16,64]{4,3,2,1,0:T(8,128)(2,1)S(1)}, bf16[1,1,16,16,64]{4,3,2,1,0:T(8,128)(2,1)S(1)}, u32[]{:S(2)}, u32[]{:S(2)}) collective-permute-start(bf16[1,1,16,16,64]{4,3,2,1,0:T(8,128)(2,1)S(1)} %get-tuple-element.82), channel_id=1, source_target_pairs={{0,16},{16,32},{32,48},{48,64},{64,80},{80,96},{96,112},{112,128},... | collective-permute-start | bytes 98312 | tf_op jit(solution)/shard_map/ppermute | solution.py:14
  6.2 5.5 %collective-permute-start.1 = (bf16[1,1,16,16,64]{4,3,2,1,0:T(8,128)(2,1)S(1)}, bf16[1,1,16,16,64]{4,3,2,1,0:T(8,128)(2,1)S(1)}, u32[]{:S(2)}, u32[]{:S(2)}) collective-permute-start(bf16[1,1,16,16,64]{4,3,2,1,0:T(8,128)(2,1)S(1)} %get-tuple-element.83), channel_id=1, source_target_pairs={{16,0},{32,16},{48,32},{64,48},{80,64},{96,80},{112,96},{128,112},... | collective-permute-start | bytes 98312 | tf_op jit(solution)/shard_map/ppermute | solution.py:15
  13.2 5.5 %all-to-all-start.2 = ((bf16[16,2,256]{2,1,0:T(2,128)(2,1)}), bf16[16,2,256]{2,1,0:T(2,128)(2,1)S(1)}, u32[]{:S(2)}, u32[]{:S(2)}) async-start(bf16[16,2,256]{2,1,0:T(2,128)(2,1)} %reshape.486), calls=%async_computation.2 | async-start | bytes 32768 | tf_op jit(solution)/shard_map/all_to_all | solution.py:188
  20.3 1.7 rev.7
  24.4 3.2 %all-to-all-done.2 = bf16[16,2,256]{2,1,0:T(2,128)(2,1)S(1)} async-done(((bf16[16,2,256]{2,1,0:T(2,128)(2,1)}), bf16[16,2,256]{2,1,0:T(2,128)(2,1)S(1)}, u32[]{:S(2)}, u32[]{:S(2)}) %all-to-all-start.2) | async-done | bytes 16416 | tf_op jit(solution)/shard_map/all_to_all | solution.py:188
  28.6 5.9 %all-to-all-start = ((bf16[16,3456,8]{1,2,0:T(8,128)(2,1)}), bf16[16,3456,8]{1,2,0:T(8,128)(2,1)S(1)}, u32[]{:S(2)}, u32[]{:S(2)}) async-start(bf16[16,3456,8]{1,2,0:T(8,128)(2,1)} %broadcast_in_dim.6), calls=%async_computation | async-start | bytes 1769472 | tf_op jit(solution)/shard_map/all_to_all | solution.py:28
  37.2 1.9 fusion.36
  39.1 1.6 pad_maximum_fusion.5
  42.2 1.9 convolution_add_fusion.3
  47.3 3.9 %collective-permute-start.2 = (bf16[1,1,8,8,128]{4,3,2,1,0:T(8,128)(2,1)S(1)}, bf16[1,1,8,8,128]{4,3,2,1,0:T(8,128)(2,1)}, u32[]{:S(2)}, u32[]{:S(2)}) collective-permute-start(bf16[1,1,8,8,128]{4,3,2,1,0:T(8,128)(2,1)S(1)} %bitcast.349), channel_id=1, source_target_pairs={{0,16},{16,32},{32,48},{48,64},{64,80},{80,96},{96,112},{112,128},... | collective-permute-start | bytes 49160 | tf_op jit(solution)/shard_map/ppermute | solution.py:14
  51.2 1.9 collective-permute-start.3
  54.3 1.8 copy.139
  68.0 1.8 fusion.52
  69.8 3.6 %collective-permute-start.4 = (bf16[1,1,8,8,128]{4,3,2,1,0:T(8,128)(2,1)}, bf16[1,1,8,8,128]{4,3,2,1,0:T(8,128)(2,1)}, u32[]{:S(2)}, u32[]{:S(2)}) collective-permute-start(bf16[1,1,8,8,128]{4,3,2,1,0:T(8,128)(2,1)} %get-tuple-element.125), channel_id=1, source_target_pairs={{0,16},{16,32},{32,48},{48,64},{64,80},{80,96},{96,112},{112,128},... | collective-permute-start | bytes 49160 | tf_op jit(solution)/shard_map/ppermute | solution.py:14
  73.4 1.9 collective-permute-start.5
  77.2 2.0 fusion.2
  80.1 5.8 %rev.6 = bf16[3,3,3,128,128]{3,2,1,0,4:T(4,128)(2,1)S(1)} reverse(bf16[3,3,3,128,128]{3,2,1,0,4:T(4,128)(2,1)} %reshape_reshape.3), dimensions={0,1,2} | reverse | bytes 1769472 | tf_op jit(solution)/shard_map/rev | solution.py:103
  90.8 10.0 %all-to-all-start.1 = ((bf16[16,2,256]{2,1,0:T(2,128)(2,1)}), bf16[16,2,256]{2,1,0:T(2,128)(2,1)S(1)}, u32[]{:S(2)}, u32[]{:S(2)}) async-start(bf16[16,2,256]{2,1,0:T(2,128)(2,1)} %reshape.488), calls=%async_computation.1 | async-start | bytes 32768 | tf_op jit(solution)/shard_map/all_to_all | solution.py:187
  105.0 4.7 %all-to-all-done.1 = bf16[16,2,256]{2,1,0:T(2,128)(2,1)S(1)} async-done(((bf16[16,2,256]{2,1,0:T(2,128)(2,1)}), bf16[16,2,256]{2,1,0:T(2,128)(2,1)S(1)}, u32[]{:S(2)}, u32[]{:S(2)}) %all-to-all-start.1) | async-done | bytes 16416 | tf_op jit(solution)/shard_map/all_to_all | solution.py:187
  109.7 4.4 %all-to-all-start.3 = ((bf16[16,3456,8]{1,2,0:T(8,128)(2,1)}), bf16[16,3456,8]{1,2,0:T(8,128)(2,1)S(1)}, u32[]{:S(2)}, u32[]{:S(2)}) async-start(bf16[16,3456,8]{1,2,0:T(8,128)(2,1)} %copy.128), calls=%async_computation.3 | async-start | bytes 1769472 | tf_op jit(solution)/shard_map/all_to_all | solution.py:44
  116.0 4.0 %collective-permute-start.6 = (bf16[1,1,16,16,64]{4,3,2,1,0:T(8,128)(2,1)}, bf16[1,1,16,16,64]{4,3,2,1,0:T(8,128)(2,1)}, u32[]{:S(2)}, u32[]{:S(2)}) collective-permute-start(bf16[1,1,16,16,64]{4,3,2,1,0:T(8,128)(2,1)} %get-tuple-element.78), channel_id=1, source_target_pairs={{0,16},{16,32},{32,48},{48,64},{64,80},{80,96},{96,112},{112,128},... | collective-permute-start | bytes 98312 | tf_op jit(solution)/shard_map/ppermute | solution.py:14
  120.0 2.1 collective-permute-start.7
  127.4 12.2 %all-to-all-done.3 = bf16[16,3456,8]{1,2,0:T(8,128)(2,1)S(1)} async-done(((bf16[16,3456,8]{1,2,0:T(8,128)(2,1)}), bf16[16,3456,8]{1,2,0:T(8,128)(2,1)S(1)}, u32[]{:S(2)}, u32[]{:S(2)}) %all-to-all-start.3) | async-done | bytes 884768 | tf_op jit(solution)/shard_map/all_to_all | solution.py:44
  140.7 15.5 %all-to-all-start.4 = ((bf16[32,56,128]{2,1,0:T(8,128)(2,1)}), bf16[32,56,128]{2,1,0:T(8,128)(2,1)S(1)}, u32[]{:S(2)}, u32[]{:S(2)}) async-start(bf16[32,56,128]{2,1,0:T(8,128)(2,1)} %pad_maximum_fusion.1), calls=%async_computation.4 | async-start | bytes 917504 | tf_op jit(solution)/shard_map/all_to_all | solution.py:150
  157.3 1.7 copy.109
  159.0 1.6 copy.110
  166.6 4.7 %all-to-all-done.4 = bf16[32,56,128]{2,1,0:T(8,128)(2,1)S(1)} async-done(((bf16[32,56,128]{2,1,0:T(8,128)(2,1)}), bf16[32,56,128]{2,1,0:T(8,128)(2,1)S(1)}, u32[]{:S(2)}, u32[]{:S(2)}) %all-to-all-start.4) | async-done | bytes 458784 | tf_op jit(solution)/shard_map/all_to_all | solution.py:150
  172.1 3.5 %all-to-all-start.5 = ((bf16[16,48,128]{2,1,0:T(8,128)(2,1)}), bf16[16,48,128]{2,1,0:T(8,128)(2,1)S(1)}, u32[]{:S(2)}, u32[]{:S(2)}) async-start(bf16[16,48,128]{2,1,0:T(8,128)(2,1)} %broadcast_in_dim.7), calls=%async_computation.5 | async-start | bytes 393216 | tf_op jit(solution)/shard_map/all_to_all | solution.py:28
  176.7 1.6 pad_maximum_fusion.3
  179.2 7.2 %all-to-all-done.5 = bf16[16,48,128]{2,1,0:T(8,128)(2,1)S(1)} async-done(((bf16[16,48,128]{2,1,0:T(8,128)(2,1)}), bf16[16,48,128]{2,1,0:T(8,128)(2,1)S(1)}, u32[]{:S(2)}, u32[]{:S(2)}) %all-to-all-start.5) | async-done | bytes 196640 | tf_op jit(solution)/shard_map/all_to_all | solution.py:28
  187.3 6.7 %all-to-all-start.6 = ((bf16[32,56,128]{2,1,0:T(8,128)(2,1)}), bf16[32,56,128]{2,1,0:T(8,128)(2,1)S(1)}, u32[]{:S(2)}, u32[]{:S(2)}) async-start(bf16[32,56,128]{2,1,0:T(8,128)(2,1)} %broadcast_in_dim.8), calls=%async_computation.6 | async-start | bytes 917504 | tf_op jit(solution)/shard_map/all_to_all | solution.py:28
  199.6 9.5 %all-to-all-done.6 = bf16[32,56,128]{2,1,0:T(8,128)(2,1)S(1)} async-done(((bf16[32,56,128]{2,1,0:T(8,128)(2,1)}), bf16[32,56,128]{2,1,0:T(8,128)(2,1)S(1)}, u32[]{:S(2)}, u32[]{:S(2)}) %all-to-all-start.6) | async-done | bytes 458784 | tf_op jit(solution)/shard_map/all_to_all | solution.py:28
  (242 shorter events, 66.2 us)
Async XLA Ops:
  0.6 46.5 %copy-start = (bf16[512,128]{1,0:T(8,128)(2,1)S(1)}, bf16[512,128]{1,0:T(8,128)(2,1)}, u32[]{:S(2)}) copy-start(bf16[512,128]{1,0:T(8,128)(2,1)} %param.8) | copy-start | bytes 393220
  1.7 32.9 %collective-permute-start = (bf16[1,1,16,16,64]{4,3,2,1,0:T(8,128)(2,1)S(1)}, bf16[1,1,16,16,64]{4,3,2,1,0:T(8,128)(2,1)S(1)}, u32[]{:S(2)}, u32[]{:S(2)}) collective-permute-start(bf16[1,1,16,16,64]{4,3,2,1,0:T(8,128)(2,1)S(1)} %get-tuple-element.82), channel_id=1, source_target_pairs={{0,16},{16,32},{32,48},{48,64},{64,80},{80,96},{96,112},{112,128},... | collective-permute-start | bytes 98312 | tf_op jit(solution)/shard_map/ppermute | solution.py:14
  6.2 28.4 %collective-permute-start.1 = (bf16[1,1,16,16,64]{4,3,2,1,0:T(8,128)(2,1)S(1)}, bf16[1,1,16,16,64]{4,3,2,1,0:T(8,128)(2,1)S(1)}, u32[]{:S(2)}, u32[]{:S(2)}) collective-permute-start(bf16[1,1,16,16,64]{4,3,2,1,0:T(8,128)(2,1)S(1)} %get-tuple-element.83), channel_id=1, source_target_pairs={{16,0},{32,16},{48,32},{64,48},{80,64},{96,80},{112,96},{128,112},... | collective-permute-start | bytes 98312 | tf_op jit(solution)/shard_map/ppermute | solution.py:15
  13.2 14.4 %all-to-all-start.2 = ((bf16[16,2,256]{2,1,0:T(2,128)(2,1)}), bf16[16,2,256]{2,1,0:T(2,128)(2,1)S(1)}, u32[]{:S(2)}, u32[]{:S(2)}) async-start(bf16[16,2,256]{2,1,0:T(2,128)(2,1)} %reshape.486), calls=%async_computation.2 | async-start | bytes 32768 | tf_op jit(solution)/shard_map/all_to_all | solution.py:188
  22.0 5.6 %copy-start.39 = (bf16[3456,8]{0,1:T(8,128)(2,1)S(1)}, bf16[3456,8]{0,1:T(8,128)(2,1)}, u32[]{:S(2)}) copy-start(bf16[3456,8]{0,1:T(8,128)(2,1)} %param.9) | copy-start | bytes 165892
  28.6 38.0 %all-to-all-start = ((bf16[16,3456,8]{1,2,0:T(8,128)(2,1)}), bf16[16,3456,8]{1,2,0:T(8,128)(2,1)S(1)}, u32[]{:S(2)}, u32[]{:S(2)}) async-start(bf16[16,3456,8]{1,2,0:T(8,128)(2,1)} %broadcast_in_dim.6), calls=%async_computation | async-start | bytes 1769472 | tf_op jit(solution)/shard_map/all_to_all | solution.py:28
  36.6 2.5 %copy-start.5 = (bf16[1,2,16,16,64]{4,3,2,1,0:T(8,128)(2,1)}, bf16[1,2,16,16,64]{4,3,2,1,0:T(8,128)(2,1)S(1)}, u32[]{:S(2)}) copy-start(bf16[1,2,16,16,64]{4,3,2,1,0:T(8,128)(2,1)S(1)} %get-tuple-element.61) | copy-start | bytes 196612
  40.7 3.3 %copy-start.23 = (bf16[1,2,16,16,64]{4,3,2,1,0:T(8,128)(2,1)S(1)}, bf16[1,2,16,16,64]{4,3,2,1,0:T(8,128)(2,1)}, u32[]{:S(2)}) copy-start(bf16[1,2,16,16,64]{4,3,2,1,0:T(8,128)(2,1)} %get-tuple-element.52) | copy-start | bytes 196612
  40.7 3.3 %copy-start.24 = (bf16[1,2,16,16,64]{4,3,2,1,0:T(8,128)(2,1)S(1)}, bf16[1,2,16,16,64]{4,3,2,1,0:T(8,128)(2,1)}, u32[]{:S(2)}) copy-start(bf16[1,2,16,16,64]{4,3,2,1,0:T(8,128)(2,1)} %get-tuple-element.53) | copy-start | bytes 196612
  40.8 3.3 %copy-start.25 = (bf16[1,2,16,16,64]{4,3,2,1,0:T(8,128)(2,1)S(1)}, bf16[1,2,16,16,64]{4,3,2,1,0:T(8,128)(2,1)}, u32[]{:S(2)}) copy-start(bf16[1,2,16,16,64]{4,3,2,1,0:T(8,128)(2,1)} %get-tuple-element.54) | copy-start | bytes 196612
  40.8 3.3 %copy-start.26 = (bf16[1,2,16,16,64]{4,3,2,1,0:T(8,128)(2,1)S(1)}, bf16[1,2,16,16,64]{4,3,2,1,0:T(8,128)(2,1)}, u32[]{:S(2)}) copy-start(bf16[1,2,16,16,64]{4,3,2,1,0:T(8,128)(2,1)} %get-tuple-element.55) | copy-start | bytes 196612
  46.7 6.5 %copy-start.12 = (f32[512,64]{0,1:T(8,128)}, f32[512,64]{0,1:T(8,128)S(1)}, u32[]{:S(2)}) copy-start(f32[512,64]{0,1:T(8,128)S(1)} %convolution_add_fusion.2) | copy-start | bytes 393220
  47.2 6.0 %copy-start.17 = (bf16[64,512]{1,0:T(8,128)(2,1)}, bf16[64,512]{1,0:T(8,128)(2,1)S(1)}, u32[]{:S(2)}) copy-start(bf16[64,512]{1,0:T(8,128)(2,1)S(1)} %reshape.441) | copy-start | bytes 196612
  47.3 11.2 %collective-permute-start.2 = (bf16[1,1,8,8,128]{4,3,2,1,0:T(8,128)(2,1)S(1)}, bf16[1,1,8,8,128]{4,3,2,1,0:T(8,128)(2,1)}, u32[]{:S(2)}, u32[]{:S(2)}) collective-permute-start(bf16[1,1,8,8,128]{4,3,2,1,0:T(8,128)(2,1)S(1)} %bitcast.349), channel_id=1, source_target_pairs={{0,16},{16,32},{32,48},{48,64},{64,80},{80,96},{96,112},{112,128},... | collective-permute-start | bytes 49160 | tf_op jit(solution)/shard_map/ppermute | solution.py:14
  51.2 7.3 %collective-permute-start.3 = (bf16[1,1,8,8,128]{4,3,2,1,0:T(8,128)(2,1)S(1)}, bf16[1,1,8,8,128]{4,3,2,1,0:T(8,128)(2,1)}, u32[]{:S(2)}, u32[]{:S(2)}) collective-permute-start(bf16[1,1,8,8,128]{4,3,2,1,0:T(8,128)(2,1)S(1)} %bitcast.350), channel_id=1, source_target_pairs={{16,0},{32,16},{48,32},{64,48},{80,64},{96,80},{112,96},{128,112},... | collective-permute-start | bytes 49160 | tf_op jit(solution)/shard_map/ppermute | solution.py:15
  58.5 9.5 %copy-start.40 = (f32[1,1,8,8,128]{4,3,2,1,0:T(8,128)S(1)}, f32[1,1,8,8,128]{4,3,2,1,0:T(8,128)}, u32[]{:S(2)}) copy-start(f32[1,1,8,8,128]{4,3,2,1,0:T(8,128)} %copy.139) | copy-start | bytes 98308
  69.8 7.1 %copy-start.28 = (f32[64,128]{1,0:T(8,128)}, f32[64,128]{1,0:T(8,128)S(1)}, u32[]{:S(2)}) copy-start(f32[64,128]{1,0:T(8,128)S(1)} %get-tuple-element.126) | copy-start | bytes 98308
  69.8 31.0 %collective-permute-start.4 = (bf16[1,1,8,8,128]{4,3,2,1,0:T(8,128)(2,1)}, bf16[1,1,8,8,128]{4,3,2,1,0:T(8,128)(2,1)}, u32[]{:S(2)}, u32[]{:S(2)}) collective-permute-start(bf16[1,1,8,8,128]{4,3,2,1,0:T(8,128)(2,1)} %get-tuple-element.125), channel_id=1, source_target_pairs={{0,16},{16,32},{32,48},{48,64},{64,80},{80,96},{96,112},{112,128},... | collective-permute-start | bytes 49160 | tf_op jit(solution)/shard_map/ppermute | solution.py:14
  73.4 27.3 %collective-permute-start.5 = (bf16[1,1,8,8,128]{4,3,2,1,0:T(8,128)(2,1)}, bf16[1,1,8,8,128]{4,3,2,1,0:T(8,128)(2,1)}, u32[]{:S(2)}, u32[]{:S(2)}) collective-permute-start(bf16[1,1,8,8,128]{4,3,2,1,0:T(8,128)(2,1)} %get-tuple-element.125), channel_id=1, source_target_pairs={{16,0},{32,16},{48,32},{64,48},{80,64},{96,80},{112,96},{128,112},... | collective-permute-start | bytes 49160 | tf_op jit(solution)/shard_map/ppermute | solution.py:15
  87.5 14.1 %copy-start.38 = (f32[64,128]{1,0:T(8,128)S(1)}, f32[64,128]{1,0:T(8,128)}, u32[]{:S(2)}) copy-start(f32[64,128]{1,0:T(8,128)} %copy.101) | copy-start | bytes 98308
  90.8 18.9 %all-to-all-start.1 = ((bf16[16,2,256]{2,1,0:T(2,128)(2,1)}), bf16[16,2,256]{2,1,0:T(2,128)(2,1)S(1)}, u32[]{:S(2)}, u32[]{:S(2)}) async-start(bf16[16,2,256]{2,1,0:T(2,128)(2,1)} %reshape.488), calls=%async_computation.1 | async-start | bytes 32768 | tf_op jit(solution)/shard_map/all_to_all | solution.py:187
  109.7 29.9 %all-to-all-start.3 = ((bf16[16,3456,8]{1,2,0:T(8,128)(2,1)}), bf16[16,3456,8]{1,2,0:T(8,128)(2,1)S(1)}, u32[]{:S(2)}, u32[]{:S(2)}) async-start(bf16[16,3456,8]{1,2,0:T(8,128)(2,1)} %copy.128), calls=%async_computation.3 | async-start | bytes 1769472 | tf_op jit(solution)/shard_map/all_to_all | solution.py:44
  114.1 8.0 %copy-start.18 = (bf16[64,512]{1,0:T(8,128)(2,1)S(1)}, bf16[64,512]{1,0:T(8,128)(2,1)}, u32[]{:S(2)}) copy-start(bf16[64,512]{1,0:T(8,128)(2,1)} %copy-done.17) | copy-start | bytes 196612
  114.3 8.7 %copy-start.1 = (bf16[1,2,16,16,64]{4,3,2,1,0:T(8,128)(2,1)}, bf16[1,2,16,16,64]{4,3,2,1,0:T(8,128)(2,1)S(1)}, u32[]{:S(2)}) copy-start(bf16[1,2,16,16,64]{4,3,2,1,0:T(8,128)(2,1)S(1)} %multiply_convert_fusion.1) | copy-start | bytes 196612
  116.0 9.1 %collective-permute-start.6 = (bf16[1,1,16,16,64]{4,3,2,1,0:T(8,128)(2,1)}, bf16[1,1,16,16,64]{4,3,2,1,0:T(8,128)(2,1)}, u32[]{:S(2)}, u32[]{:S(2)}) collective-permute-start(bf16[1,1,16,16,64]{4,3,2,1,0:T(8,128)(2,1)} %get-tuple-element.78), channel_id=1, source_target_pairs={{0,16},{16,32},{32,48},{48,64},{64,80},{80,96},{96,112},{112,128},... | collective-permute-start | bytes 98312 | tf_op jit(solution)/shard_map/ppermute | solution.py:14
  120.0 6.3 %collective-permute-start.7 = (bf16[1,1,16,16,64]{4,3,2,1,0:T(8,128)(2,1)}, bf16[1,1,16,16,64]{4,3,2,1,0:T(8,128)(2,1)}, u32[]{:S(2)}, u32[]{:S(2)}) collective-permute-start(bf16[1,1,16,16,64]{4,3,2,1,0:T(8,128)(2,1)} %get-tuple-element.79), channel_id=1, source_target_pairs={{16,0},{32,16},{48,32},{64,48},{80,64},{96,80},{112,96},{128,112},... | collective-permute-start | bytes 98312 | tf_op jit(solution)/shard_map/ppermute | solution.py:15
  123.4 3.0 %copy-start.2 = (bf16[1,2,16,16,64]{4,3,2,1,0:T(8,128)(2,1)S(1)}, bf16[1,2,16,16,64]{4,3,2,1,0:T(8,128)(2,1)}, u32[]{:S(2)}) copy-start(bf16[1,2,16,16,64]{4,3,2,1,0:T(8,128)(2,1)} %copy-done.1) | copy-start | bytes 196612
  140.7 30.6 %all-to-all-start.4 = ((bf16[32,56,128]{2,1,0:T(8,128)(2,1)}), bf16[32,56,128]{2,1,0:T(8,128)(2,1)S(1)}, u32[]{:S(2)}, u32[]{:S(2)}) async-start(bf16[32,56,128]{2,1,0:T(8,128)(2,1)} %pad_maximum_fusion.1), calls=%async_computation.4 | async-start | bytes 917504 | tf_op jit(solution)/shard_map/all_to_all | solution.py:150
  157.3 8.3 %copy-start.13 = (f32[512,64]{0,1:T(8,128)S(1)}, f32[512,64]{0,1:T(8,128)}, u32[]{:S(2)}) copy-start(f32[512,64]{0,1:T(8,128)} %copy-done.12) | copy-start | bytes 393220
  172.1 14.3 %all-to-all-start.5 = ((bf16[16,48,128]{2,1,0:T(8,128)(2,1)}), bf16[16,48,128]{2,1,0:T(8,128)(2,1)S(1)}, u32[]{:S(2)}, u32[]{:S(2)}) async-start(bf16[16,48,128]{2,1,0:T(8,128)(2,1)} %broadcast_in_dim.7), calls=%async_computation.5 | async-start | bytes 393216 | tf_op jit(solution)/shard_map/all_to_all | solution.py:28
  179.2 14.8 %copy-start.27 = (bf16[1,2,16,16,64]{4,3,2,1,0:T(8,128)(2,1)S(1)}, bf16[1,2,16,16,64]{4,3,2,1,0:T(8,128)(2,1)}, u32[]{:S(2)}) copy-start(bf16[1,2,16,16,64]{4,3,2,1,0:T(8,128)(2,1)} %get-tuple-element.36) | copy-start | bytes 196612
  187.3 21.8 %all-to-all-start.6 = ((bf16[32,56,128]{2,1,0:T(8,128)(2,1)}), bf16[32,56,128]{2,1,0:T(8,128)(2,1)S(1)}, u32[]{:S(2)}, u32[]{:S(2)}) async-start(bf16[32,56,128]{2,1,0:T(8,128)(2,1)} %broadcast_in_dim.8), calls=%async_computation.6 | async-start | bytes 917504 | tf_op jit(solution)/shard_map/all_to_all | solution.py:28
  (24 other events, 42.0 us)

commit v2 on v0

v2 whole, which is shorter than its diff:
```python
import jax
import jax.numpy as jnp
from jax import lax
from jax.experimental import pallas as pl
from jax.experimental.pallas import tpu as pltpu
from jax.sharding import PartitionSpec as P

F32 = jnp.float32
BF16 = jnp.bfloat16
NN = (((1,), (0,)), ((), ()))
NT = (((1,), (1,)), ((), ()))
TN = (((0,), (0,)), ((), ()))


def mm(left, right, dims):
    return lax.dot_general(left, right, dims, preferred_element_type=F32)


def shift_rows(value, by, period):
    total = value.shape[0]
    place = lax.broadcasted_iota(jnp.int32, value.shape, 0) % period
    inside = place != (0 if by == 1 else period - 1)
    return jnp.where(inside, pltpu.roll(value, by % total, 0), 0.0)


def low_half(rows):
    return lax.broadcasted_iota(jnp.int32, (rows, 128), 1) < 64


def slope_and_silu(pre):
    sig = jax.nn.sigmoid(pre)
    return sig * (1.0 + pre * (1.0 - sig)), pre * sig


def fill_windows(windows, plane, blocks):
    low = low_half(16)
    none = jnp.zeros((16, 128), BF16)
    for j in range(8):
        after = blocks[j + 1] if j < 7 else none
        before = blocks[j - 1] if j > 0 else none
        rows = pl.ds(j * 16, 16)
        windows[plane, rows, 0:128] = blocks[j]
        windows[plane, rows, 128:256] = jnp.where(low, after, before)


def window_conv(windows, weights, dims):
    parts = []
    for dx in range(3):
        total = None
        for dz in range(3):
            rows = windows[dz : dz + 2].reshape(256, 256)
            term = mm(rows, weights[dz * 3 + dx], dims)
            total = term if total is None else total + term
        parts.append(total)
    return parts[1] + shift_rows(parts[0], 1, 16) + shift_rows(parts[2], -1, 16)


def place_weights(kernel, ahead, behind):
    low = low_half(64)
    tiles = [kernel[:, m * 128 : (m + 1) * 128].astype(F32) for m in range(13)]
    last = kernel[:, 1664:1728].astype(F32)
    tiles.append(jnp.concatenate([last, jnp.zeros((64, 64), F32)], axis=1))
    for k in range(9):
        first, second = tiles[3 * k // 2], tiles[3 * k // 2 + 1]
        swapped = pltpu.roll(jnp.where(low, second, first), 64, 1)
        if k % 2 == 0:
            zero_one, two_none = first, jnp.where(low, second, 0.0)
            one_two, none_zero = swapped, pltpu.roll(jnp.where(low, first, 0.0), 64, 1)
        else:
            one_two, none_zero = second, jnp.where(low, 0.0, first)
            zero_one, two_none = swapped, pltpu.roll(jnp.where(low, 0.0, second), 64, 1)
        blocks = [part.astype(BF16) for part in (one_two, zero_one, none_zero, two_none)]
        ahead[k, 0:64, 0:128] = blocks[0]
        ahead[k, 64:128, 0:128] = blocks[1]
        ahead[k, 0:64, 128:256] = blocks[2]
        ahead[k, 64:128, 128:256] = blocks[3]
        for slot in range(4):
            behind[8 - k, slot * 64 : (slot + 1) * 64] = blocks[slot]


def fine_forward(vol, before, after, weights, down, coarse, slope, windows, pooled, act):
    def lanes(ref, j):
        return ref[:, j * 128 : (j + 1) * 128]

    fill_windows(windows, 0, [lanes(before, j) for j in range(8)])
    fill_windows(windows, 1, [vol[0, :, j * 128 : (j + 1) * 128] for j in range(8)])
    fill_windows(windows, 2, [vol[1, :, j * 128 : (j + 1) * 128] for j in range(8)])
    fill_windows(windows, 3, [lanes(after, j) for j in range(8)])
    pre = window_conv(windows, weights, NT)
    slopes, silu = slope_and_silu(pre)
    slope[...] = slopes
    act[...] = silu
    for z in range(2):
        for bx in range(2):
            part = act[pl.ds(z * 128 + bx, 64, stride=2), :]
            at = (z * 2 + bx) * 128
            pooled[:, at : at + 128] = part.astype(BF16)
    coarse[...] = mm(pooled[...], down[...], NN).astype(BF16)


def y_taps(plane):
    value = plane[...].astype(F32)
    edge = jnp.zeros((8, 128), F32)
    earlier = jnp.concatenate([edge, value[:-8]], axis=0)
    later = jnp.concatenate([value[8:], edge], axis=0)
    return jnp.concatenate([earlier, value, later], axis=1).astype(BF16)


def coarse_forward(own, before, after, packed, grad, out, scratch):
    planes = [y_taps(before), y_taps(own), y_taps(after)]
    parts = []
    for dx in range(3):
        total = None
        for dz in range(3):
            at = (dz * 3 + dx) * 384
            term = mm(planes[dz], packed[:, at : at + 384], NT)
            total = term if total is None else total + term
        parts.append(total)
    pre = parts[1] + shift_rows(parts[0], 1, 8) + shift_rows(parts[2], -1, 8)
    slopes, silu = slope_and_silu(pre)
    scratch[0:64] = silu
    by_x = [scratch[pl.ds(x, 8, stride=8), :] for x in range(8)]
    ordered = jnp.concatenate(by_x + [jnp.zeros((64, 128), F32)], axis=0)
    out[...] = ordered.T.astype(BF16)
    scratch[...] = packed[:, 3456:3584].astype(F32).T
    cotangent = jnp.concatenate([scratch[pl.ds(y, 8, stride=8), :] for y in range(8)], axis=0)
    grad[...] = (cotangent * slopes).astype(BF16)


def coarse_kernel_terms(own, before, after, grad, terms):
    value = grad[...].astype(F32)
    moved = [shift_rows(value, -1, 8), value, shift_rows(value, 1, 8)]
    moved = jnp.concatenate(moved, axis=1).astype(BF16)
    for dz, plane in enumerate((before, own, after)):
        block = mm(moved, y_taps(plane), TN)
        for dx in range(3):
            for dy in range(3):
                part = block[dx * 128 : (dx + 1) * 128, dy * 128 : (dy + 1) * 128]
                terms[(dz * 3 + dx) * 3 + dy] = part.astype(BF16)
    for spare in range(27, 32):
        terms[spare] = jnp.zeros((128, 128), BF16)


def backward(own, before, after, packed, pooled, slope, windows, down, shared, fine_grad, act):
    planes = [after[...], own[...], before[...]]
    edge = jnp.zeros((8, 128), F32)
    parts = []
    for dx in range(3):
        total = None
        for dz in range(3):
            at = (dz * 3 + dx) * 384
            term = mm(planes[dz], packed[:, at : at + 384], NN)
            total = term if total is None else total + term
        earlier = jnp.concatenate([total[8:, 0:128], edge], axis=0)
        later = jnp.concatenate([edge, total[:-8, 256:384]], axis=0)
        parts.append(earlier + total[:, 128:256] + later)
    in_grad = parts[1] + shift_rows(parts[0], -1, 8) + shift_rows(parts[2], 1, 8)
    in_grad = in_grad.astype(BF16)
    act_grad = mm(in_grad, down[...], NT)
    for z in range(2):
        for bx in range(2):
            at = (z * 2 + bx) * 128
            act[pl.ds(z * 128 + bx, 64, stride=2), :] = act_grad[:, at : at + 128]
    grad = (act[...] * slope[...]).astype(BF16)
    fine_grad[0] = grad[0:128]
    fine_grad[1] = grad[128:256]
    value = grad.astype(F32)
    moved = [shift_rows(value, -1, 16), value, shift_rows(value, 1, 16)]
    moved = [part.astype(BF16) for part in moved]
    low = low_half(64)
    held = None
    for dz in range(3):
        rows = windows[dz : dz + 2].reshape(256, 256)
        for dx in range(3):
            block = mm(moved[dx], rows, TN)
            u0, u1 = block[0:64, 0:128], block[0:64, 128:256]
            v0, v1 = block[64:128, 0:128], block[64:128, 128:256]
            for dy, (left, right) in enumerate(((u1, v0), (v0, u0), (u0, v1))):
                tap = (dz * 3 + dx) * 3 + dy
                if tap % 2 == 0:
                    held = pltpu.roll(left, 64, 1) + right
                else:
                    high = left + pltpu.roll(right, 64, 1)
                    at = (tap // 2) * 64
                    shared[at : at + 64] = jnp.where(low, held, high).astype(BF16)
    shared[832:896] = jnp.where(low, held, 0.0).astype(BF16)
    shared[896:1408] = mm(pooled[...], in_grad, TN).astype(BF16)
    shared[1408:1536] = jnp.zeros((128, 128), BF16)


def fine_backward(grad, before, after, weights, out, windows):
    def blocks(plane):
        return [plane[j * 16 : (j + 1) * 16] for j in range(8)]

    fill_windows(windows, 0, blocks(before[...]))
    fill_windows(windows, 1, blocks(grad[0]))
    fill_windows(windows, 2, blocks(grad[1]))
    fill_windows(windows, 3, blocks(after[...]))
    total = window_conv(windows, weights, NN).astype(BF16)
    for z in range(2):
        for j in range(8):
            at = z * 128 + j * 16
            out[z, :, j * 128 : (j + 1) * 128] = total[at : at + 16]


def sum_slabs(terms, shared, features, out):
    def total(ref, at):
        return jnp.sum(ref[:, at : at + 16, :].astype(F32), axis=0)

    for pair in range(8):
        both = total(terms, pair * 16)
        for half in range(2):
            at = pair * 2 + half
            rows = [both[half * 8 : half * 8 + 8], features[at * 8 : at * 8 + 8].astype(F32)]
            out[at, 0:16] = jnp.concatenate(rows, axis=0).astype(BF16)
    for part in range(3):
        rows = total(shared, part * 16).astype(BF16)
        for at in range(16):
            out[at, 16 + part * 16 : 32 + part * 16] = rows


def sum_groups(parts, features, out):
    mixed = parts[:, 0:16, :].astype(F32)
    own = jnp.sum(mixed[:, 0:8], axis=0).astype(BF16)
    for at in range(16):
        features[at] = mixed[at, 8:16, 0:64].astype(BF16)
    rows = [
        jnp.sum(parts[:, 16 + part * 16 : 32 + part * 16, :].astype(F32), axis=0).astype(BF16)
        for part in range(3)
    ]
    for at in range(32):
        for part in range(3):
            out[at, part * 16 : part * 16 + 16] = rows[part]
        out[at, 48:56] = own


def unpack(parts, fine, down, coarse):
    shared = parts[:, 0:48, :].astype(F32).reshape(1536, 128)
    for tile in range(13):
        fine[:, tile * 128 : (tile + 1) * 128] = shared[tile * 64 : (tile + 1) * 64]
    fine[:, 1664:1728] = shared[832:896, 0:64]
    down[...] = shared[896:1408]
    for tap in range(27):
        coarse[:, tap * 128 : (tap + 1) * 128] = parts[tap, 48:56, :].astype(F32)


def call(body, name, outs, *operands, scratch=()):
    return pl.pallas_call(
        body,
        out_shape=[jax.ShapeDtypeStruct(shape, kind) for shape, kind in outs],
        scratch_shapes=[pltpu.VMEM(shape, kind) for shape, kind in scratch],
        name=name,
        cost_estimate=pl.CostEstimate(flops=WORK, transcendentals=0, bytes_accessed=1 << 20),
        interpret=INTERPRET,
    )(*operands)


INTERPRET = False
WORK = 250_000_000


def from_sides(last, first):
    devices = lax.axis_size("gz")
    up = [(i, i + 1) for i in range(devices - 1)]
    down = [(j, i) for i, j in up]
    return lax.ppermute(last, "gz", up), lax.ppermute(first, "gz", down)


def exchange(blocks, axis):
    return lax.all_to_all(blocks, axis, 0, 0, tiled=True)


def per_device(volumes, cotangent, fine_kernel, down_kernel, coarse_kernel):
    group = lax.axis_size("grp")
    slabs = lax.axis_size("gz")
    vol = volumes[0]
    before, after = from_sides(vol[1], vol[0])
    kernel_rows = jnp.broadcast_to(coarse_kernel.T[None], (group, 8, 3456))
    cot_rows = jnp.pad(jnp.swapaxes(cotangent[:, 0], 1, 2), ((0, 0), (0, 0), (0, 64)))
    packed = exchange(jnp.concatenate([kernel_rows, cot_rows], axis=2), "grp").reshape(128, 3584)
    ahead, behind = call(
        place_weights,
        "place_weights",
        [((9, 128, 256), BF16), ((9, 256, 128), BF16)],
        fine_kernel.T,
    )

    coarse_in, slope, windows, pooled = call(
        fine_forward,
        "fine_forward",
        [((64, 128), BF16), ((256, 128), F32), ((4, 128, 256), BF16), ((64, 512), BF16)],
        vol, before, after, ahead, down_kernel,
        scratch=[((256, 128), F32)],
    )
    in_before, in_after = from_sides(coarse_in, coarse_in)
    coarse_grad, features = call(
        coarse_forward,
        "coarse_forward",
        [((64, 128), BF16), ((128, 128), BF16)],
        coarse_in, in_before, in_after, packed,
        scratch=[((128, 128), F32)],
    )
    grad_before, grad_after = from_sides(coarse_grad, coarse_grad)
    (terms,) = call(
        coarse_kernel_terms,
        "coarse_kernel_terms",
        [((slabs, 128, 128), BF16)],
        coarse_in, in_before, in_after, coarse_grad,
    )
    grad_before, grad_after, terms = lax.optimization_barrier((grad_before, grad_after, terms))
    terms = exchange(terms, "gz")
    shared, fine_grad = call(
        backward,
        "backward",
        [((1536, 128), BF16), ((2, 128, 128), BF16)],
        coarse_grad, grad_before, grad_after, packed, pooled, slope, windows, down_kernel,
        scratch=[((256, 128), F32)],
    )
    shared = exchange(shared.reshape(slabs, 48, 128), "gz")
    fine_before, fine_after = from_sides(fine_grad[1], fine_grad[0])
    (volume_grad,) = call(
        fine_backward,
        "fine_backward",
        [((2, 16, 1024), BF16)],
        fine_grad, fine_before, fine_after, behind,
        scratch=[((4, 128, 256), BF16)],
    )
    (parts,) = call(sum_slabs, "sum_slabs", [((group, 64, 128), BF16)], terms, shared, features)
    parts = exchange(parts, "grp")
    out_rows, final = call(
        sum_groups, "sum_groups", [((group, 8, 64), BF16), ((slabs, 56, 128), BF16)], parts
    )
    final = exchange(final, "gz")
    fine_kg, down_kg, coarse_kg = call(
        unpack, "unpack", [((64, 1728), F32), ((512, 128), F32), ((8, 3456), F32)], final
    )
    coarse_out = jnp.swapaxes(out_rows, 1, 2)[:, None]
    return (coarse_out, volume_grad[None], fine_kg.T, down_kg, coarse_kg.T)


def solution(mesh):
    in_specs = (P("grp", "gz", None, None), P(None, "gz", None, "grp"), P(), P(), P(None, "grp"))
    out_specs = (P(None, "gz", None, "grp"), P("grp", "gz", None, None), P(), P(), P(None, "grp"))
    return jax.shard_map(
        per_device, mesh=mesh, in_specs=in_specs, out_specs=out_specs, check_vma=False
    )
```

time: 438 us -> 162 us (0.37)
  waiting for transfers between devices: 276 us -> 14.7 us
  blocking collectives: 0 us -> 75.9 us
  local copies, waits for them, and re-layouts: 67.7 us -> 4.41 us
  Pallas kernels: 0 us -> 20.5 us
  between operations: 16.5 us -> 0.79 us
  matrix products: 13.5 us -> 0 us
  starting transfers between devices: 52.6 us -> 42.5 us
  other arithmetic: 10.1 us -> 1.76 us
    psum x1 -> x0, waiting for transfers between devices: 220 us -> none  [per_device(): fine_kg, down_kg = lax.psum((fine_kg, down_kg), ('gz', 'grp'))]
    all_to_all x0 -> x3, blocking collectives: none -> 75.9 us  [exchange(): return lax.all_to_all(blocks, axis, 0, 0, tiled=True)]
    all_gather x1 -> x0, waiting for transfers between devices: 41.3 us -> none  [total_of_pieces(): parts = lax.all_gather(array, axis).astype(jnp.float32)]
    pallas_call x0 -> x9, Pallas kernels: none -> 20.5 us  [call(): pl.pallas_call(body, out_shape=[jax.ShapeDtypeStruct(shape, kind) for sha...]
    concatenate x22 -> x0, local copies, waits for them, and re-layouts: 17.8 us -> none  [the longest x21 16.9 us: convolve(): columns = jnp.concatenate(pieces, axis=-1).reshape(-1, 9 * channels)]
    unnamed x119 -> x26, local copies, waits for them, and re-layouts: 20.8 us -> 3.52 us
    dot_general x21 -> x0, matrix products: 13.5 us -> none  [the longest x12 10.5 us: convolve(): partial_value = jnp.dot(columns, rows, preferred_element_type=jnp.float32)]
    rev x2 -> x0, local copies, waits for them, and re-layouts: 7.54 us -> none  [flip_kernel(): shaped = kernel.reshape(3, 3, 3, inputs, outputs)[::-1, ::-1, ::-1]]
  transfers between devices with their start and end apart: 14 -> 10, of which waited for: 4 -> 5; matrix products, arithmetic and copies ran while one was open for 19% -> 0% of each run, Pallas kernels for 0% -> 6%
where the time goes in v2:
time: 162 us; the launch traced here: 161 us
  blocking collectives  75.9 us (47%)
  starting transfers between devices  42.5 us (26%)
  Pallas kernels  20.5 us (13%)
  waiting for transfers between devices  14.7 us (9%)
  local copies, waits for them, and re-layouts  4.41 us (3%)
  other arithmetic  1.76 us (1%)
    all_to_all x3, blocking collectives, exchange(): return lax.all_to_all(blocks, axis, 0, 0, tiled=True)  75.9 us
    ppermute x8, starting transfers between devices, from_sides(): return (lax.ppermute(last, 'gz', up), lax.ppermute(first, 'gz', down))  24.6 us
    pallas_call x9, Pallas kernels, call(): pl.pallas_call(body, out_shape=[jax.ShapeDtypeStruct(shape, kind) for sha...  20.5 us
    all_to_all x2, starting transfers between devices, exchange(): return lax.all_to_all(blocks, axis, 0, 0, tiled=True)  17.9 us
    all_to_all x2, waiting for transfers between devices, exchange(): return lax.all_to_all(blocks, axis, 0, 0, tiled=True)  12.6 us
    unnamed x26, local copies, waits for them, and re-layouts  3.52 us
  transfers between devices with their start and end apart: 10, of which 5 were waited for; matrix products, arithmetic and copies ran while one was open for 0% of the time, Pallas kernels for 6%

profile of v2, /device:TPU:1, one launch (start us, length us, event | category | flops | bytes accessed | tf_op | source)
XLA Modules:
  0.0 160.6 jit_solution(8745177820303363301)
XLA Ops:
  0.6 0.9 broadcast_in_dim.12
  1.5 1.8 %fusion.1 = bf16[16,8,3584]{2,1,0:T(8,128)(2,1)} fusion(bf16[16,8,64]{2,1,0:T(8,128)(2,1)} %bitcast.29, bf16[16,8,3456]{2,1,0:T(8,128)(2,1)S(1)} %broadcast_in_dim.12), kind=kLoop, calls=%fused_computation.2 | loop fusion | flops 2752512 | bytes 1818624 | tf_op jit(solution)/shard_map/concatenate | solution.py:280
  3.3 10.3 %all-to-all-start = ((bf16[16,8,3584]{2,1,0:T(8,128)(2,1)}), bf16[16,8,3584]{2,1,0:T(8,128)(2,1)S(1)}, u32[]{:S(2)}, u32[]{:S(2)}) async-start(bf16[16,8,3584]{2,1,0:T(8,128)(2,1)} %fusion.1), calls=%async_computation | async-start | bytes 1835008 | tf_op jit(solution)/shard_map/all_to_all | solution.py:270
  13.6 2.9 %collective-permute-start.1 = (bf16[16,1024]{1,0:T(8,128)(2,1)S(1)}, bf16[16,1024]{1,0:T(8,128)(2,1)S(1)}, u32[]{:S(2)}, u32[]{:S(2)}) collective-permute-start(bf16[16,1024]{1,0:T(8,128)(2,1)S(1)} %get-tuple-element.48), channel_id=1, source_target_pairs={{16,0},{32,16},{48,32},{64,48},{80,64},{96,80},{112,96},{128,112},... | collective-permute-start | bytes 98312 | tf_op jit(solution)/shard_map/ppermute | solution.py:266
  16.5 2.7 %collective-permute-start = (bf16[16,1024]{1,0:T(8,128)(2,1)S(1)}, bf16[16,1024]{1,0:T(8,128)(2,1)S(1)}, u32[]{:S(2)}, u32[]{:S(2)}) collective-permute-start(bf16[16,1024]{1,0:T(8,128)(2,1)S(1)} %get-tuple-element.49), channel_id=1, source_target_pairs={{0,16},{16,32},{32,48},{48,64},{64,80},{80,96},{96,112},{112,128},... | collective-permute-start | bytes 98312 | tf_op jit(solution)/shard_map/ppermute | solution.py:266
  19.2 2.1 %place_weights.1 = (bf16[9,128,256]{2,1,0:T(8,128)(2,1)}, bf16[9,256,128]{2,1,0:T(8,128)(2,1)}) custom-call(bf16[64,1728]{1,0:T(8,128)(2,1)} %bitcast.30), custom_call_target="tpu_custom_call" | custom-call | flops 250000000 | bytes 1048576 | tf_op jit(solution)/shard_map/place_weights/pallas_call | solution.py:248
  21.4 0.6 copy-done.9
  22.0 2.4 %fine_forward.1 = (bf16[64,128]{1,0:T(8,128)(2,1)}, f32[256,128]{1,0:T(8,128)}, bf16[4,128,256]{2,1,0:T(8,128)(2,1)}, bf16[64,512]{1,0:T(8,128)(2,1)}) custom-call(bf16[2,16,1024]{2,1,0:T(8,128)(2,1)} %bitcast.27, bf16[16,1024]{1,0:T(8,128)(2,1)} %copy-done.10, bf16[16,1024]{1,0:T(8,128)(2,1)} %copy-done.9, bf16[9,128,256]{2,1,0:T(8,128)(2,1)} %get-tuple-element.23.weights, ...), custom_call_target="tpu_custom_call" | custom-call | flops 250000000 | bytes 1048576 | tf_op jit(solution)/shard_map/fine_forward/pallas_call | solution.py:248
  24.4 1.9 %collective-permute-start.3 = (bf16[64,128]{1,0:T(8,128)(2,1)}, bf16[64,128]{1,0:T(8,128)(2,1)S(1)}, u32[]{:S(2)}, u32[]{:S(2)}) collective-permute-start(bf16[64,128]{1,0:T(8,128)(2,1)} %get-tuple-element.24.own), channel_id=1, source_target_pairs={{16,0},{32,16},{48,32},{64,48},{80,64},{96,80},{112,96},{128,112},... | collective-permute-start | bytes 49160 | tf_op jit(solution)/shard_map/ppermute | solution.py:266
  26.3 3.6 %collective-permute-start.2 = (bf16[64,128]{1,0:T(8,128)(2,1)}, bf16[64,128]{1,0:T(8,128)(2,1)S(1)}, u32[]{:S(2)}, u32[]{:S(2)}) collective-permute-start(bf16[64,128]{1,0:T(8,128)(2,1)} %get-tuple-element.24.own), channel_id=1, source_target_pairs={{0,16},{16,32},{32,48},{48,64},{64,80},{80,96},{96,112},{112,128},... | collective-permute-start | bytes 49160 | tf_op jit(solution)/shard_map/ppermute | solution.py:266
  30.0 1.0 collective-permute-done.2.before
  31.0 7.1 %all-to-all-done = bf16[16,8,3584]{2,1,0:T(8,128)(2,1)S(1)} async-done(((bf16[16,8,3584]{2,1,0:T(8,128)(2,1)}), bf16[16,8,3584]{2,1,0:T(8,128)(2,1)S(1)}, u32[]{:S(2)}, u32[]{:S(2)}) %all-to-all-start) | async-done | bytes 917536 | tf_op jit(solution)/shard_map/all_to_all | solution.py:270
  38.1 0.9 copy-done
  39.0 2.5 %coarse_forward.1 = (bf16[64,128]{1,0:T(8,128)(2,1)}, bf16[128,128]{1,0:T(8,128)(2,1)}) custom-call(bf16[64,128]{1,0:T(8,128)(2,1)} %get-tuple-element.24.own, bf16[64,128]{1,0:T(8,128)(2,1)} %copy-done.4, bf16[64,128]{1,0:T(8,128)(2,1)} %copy-done.3, bf16[128,3584]{1,0:T(8,128)(2,1)} %bitcast.24), custom_call_target="tpu_custom_call" | custom-call | flops 250000000 | bytes 1048576 | tf_op jit(solution)/shard_map/coarse_forward/pallas_call | solution.py:248
  41.5 5.7 %collective-permute-start.5 = (bf16[64,128]{1,0:T(8,128)(2,1)}, bf16[64,128]{1,0:T(8,128)(2,1)S(1)}, u32[]{:S(2)}, u32[]{:S(2)}) collective-permute-start(bf16[64,128]{1,0:T(8,128)(2,1)} %get-tuple-element.25.grad.own), channel_id=1, source_target_pairs={{16,0},{32,16},{48,32},{64,48},{80,64},{96,80},{112,96},{128,112},... | collective-permute-start | bytes 49160 | tf_op jit(solution)/shard_map/ppermute | solution.py:266
  47.2 2.1 %collective-permute-start.4 = (bf16[64,128]{1,0:T(8,128)(2,1)}, bf16[64,128]{1,0:T(8,128)(2,1)S(1)}, u32[]{:S(2)}, u32[]{:S(2)}) collective-permute-start(bf16[64,128]{1,0:T(8,128)(2,1)} %get-tuple-element.25.grad.own), channel_id=1, source_target_pairs={{0,16},{16,32},{32,48},{48,64},{64,80},{80,96},{96,112},{112,128},... | collective-permute-start | bytes 49160 | tf_op jit(solution)/shard_map/ppermute | solution.py:266
  49.3 2.2 %coarse_kernel_terms.1 = bf16[32,128,128]{2,1,0:T(8,128)(2,1)} custom-call(bf16[64,128]{1,0:T(8,128)(2,1)} %get-tuple-element.24.own, bf16[64,128]{1,0:T(8,128)(2,1)} %copy-done.4, bf16[64,128]{1,0:T(8,128)(2,1)} %copy-done.3, bf16[64,128]{1,0:T(8,128)(2,1)} %get-tuple-element.25.grad.own), custom_call_target="tpu_custom_call" | custom-call | flops 250000000 | bytes 1048576 | tf_op jit(solution)/shard_map/coarse_kernel_terms/pallas_call | solution.py:248
  52.1 3.1 %backward.1 = (bf16[1536,128]{1,0:T(8,128)(2,1)}, bf16[2,128,128]{2,1,0:T(8,128)(2,1)}) custom-call(bf16[64,128]{1,0:T(8,128)(2,1)} %get-tuple-element.25.grad.own, bf16[64,128]{1,0:T(8,128)(2,1)} %copy-done.8, bf16[64,128]{1,0:T(8,128)(2,1)} %copy-done.7, bf16[128,3584]{1,0:T(8,128)(2,1)} %bitcast.25, bf16[64,512]{1,0:T(8,128)(2,1)} %get-tuple-element.29.pooled, ...), custom_call_target="tpu_custom_call" | custom-call | flops 250000000 | bytes 1048576 | tf_op jit(solution)/shard_map/backward/pallas_call | solution.py:248
  55.2 27.3 %all_to_all.25.shared = bf16[32,48,128]{2,1,0:T(8,128)(2,1)} all-to-all(bf16[32,48,128]{2,1,0:T(8,128)(2,1)} %bitcast.26), channel_id=1, replica_groups=mesh['gz'=32,'grp'=16] {'gz'}, dimensions={0} | all-to-all | bytes 786432 | tf_op jit(solution)/shard_map/all_to_all | solution.py:270
  82.6 33.0 %all_to_all.26.terms = bf16[32,128,128]{2,1,0:T(8,128)(2,1)} all-to-all(bf16[32,128,128]{2,1,0:T(8,128)(2,1)S(1)} %copy-done.1), channel_id=1, replica_groups=mesh['gz'=32,'grp'=16] {'gz'}, dimensions={0} | all-to-all | bytes 2097152 | tf_op jit(solution)/shard_map/all_to_all | solution.py:270
  115.6 2.3 %sum_slabs.1 = bf16[16,64,128]{2,1,0:T(8,128)(2,1)} custom-call(bf16[32,128,128]{2,1,0:T(8,128)(2,1)} %all_to_all.26.terms, bf16[32,48,128]{2,1,0:T(8,128)(2,1)} %all_to_all.25.shared, bf16[128,128]{1,0:T(8,128)(2,1)} %get-tuple-element.33.features), custom_call_target="tpu_custom_call" | custom-call | flops 250000000 | bytes 1048576 | tf_op jit(solution)/shard_map/sum_slabs/pallas_call | solution.py:248
  117.9 15.5 %all_to_all.27.parts = bf16[16,64,128]{2,1,0:T(8,128)(2,1)} all-to-all(bf16[16,64,128]{2,1,0:T(8,128)(2,1)} %sum_slabs.1), channel_id=1, replica_groups=mesh['gz'=32,'grp'=16] {'grp'}, dimensions={0} | all-to-all | bytes 524288 | tf_op jit(solution)/shard_map/all_to_all | solution.py:270
  133.4 1.8 %sum_groups.1 = (bf16[16,8,64]{2,1,0:T(8,128)(2,1)}, bf16[32,56,128]{2,1,0:T(8,128)(2,1)}) custom-call(bf16[16,64,128]{2,1,0:T(8,128)(2,1)} %all_to_all.27.parts), custom_call_target="tpu_custom_call" | custom-call | flops 250000000 | bytes 1048576 | tf_op jit(solution)/shard_map/sum_groups/pallas_call | solution.py:248
  135.2 7.6 %all-to-all-start.4 = ((bf16[32,56,128]{2,1,0:T(8,128)(2,1)}), bf16[32,56,128]{2,1,0:T(8,128)(2,1)S(1)}, u32[]{:S(2)}, u32[]{:S(2)}) async-start(bf16[32,56,128]{2,1,0:T(8,128)(2,1)} %get-tuple-element.37), calls=%async_computation.4 | async-start | bytes 917504 | tf_op jit(solution)/shard_map/all_to_all | solution.py:270
  142.8 2.1 %collective-permute-start.7 = (bf16[128,128]{1,0:T(8,128)(2,1)S(1)}, bf16[128,128]{1,0:T(8,128)(2,1)S(1)}, u32[]{:S(2)}, u32[]{:S(2)}) collective-permute-start(bf16[128,128]{1,0:T(8,128)(2,1)S(1)} %get-tuple-element.46), channel_id=1, source_target_pairs={{16,0},{32,16},{48,32},{64,48},{80,64},{96,80},{112,96},{128,112},... | collective-permute-start | bytes 98312 | tf_op jit(solution)/shard_map/ppermute | solution.py:266
  145.0 3.5 %collective-permute-start.6 = (bf16[128,128]{1,0:T(8,128)(2,1)S(1)}, bf16[128,128]{1,0:T(8,128)(2,1)S(1)}, u32[]{:S(2)}, u32[]{:S(2)}) collective-permute-start(bf16[128,128]{1,0:T(8,128)(2,1)S(1)} %get-tuple-element.47), channel_id=1, source_target_pairs={{0,16},{16,32},{32,48},{48,64},{64,80},{80,96},{96,112},{112,128},... | collective-permute-start | bytes 98312 | tf_op jit(solution)/shard_map/ppermute | solution.py:266
  148.6 1.0 collective-permute-done.6.before
  149.5 0.6 copy-done.12
  150.1 2.2 %fine_backward.1 = bf16[2,16,1024]{2,1,0:T(8,128)(2,1)} custom-call(bf16[2,128,128]{2,1,0:T(8,128)(2,1)} %get-tuple-element.35.grad, bf16[128,128]{1,0:T(8,128)(2,1)} %copy-done.12, bf16[128,128]{1,0:T(8,128)(2,1)} %copy-done.11, bf16[9,256,128]{2,1,0:T(8,128)(2,1)} %get-tuple-element.36.weights), custom_call_target="tpu_custom_call" | custom-call | flops 250000000 | bytes 1048576 | tf_op jit(solution)/shard_map/fine_backward/pallas_call | solution.py:248
  152.4 5.5 %all-to-all-done.4.parts = bf16[32,56,128]{2,1,0:T(8,128)(2,1)S(1)} async-done(((bf16[32,56,128]{2,1,0:T(8,128)(2,1)}), bf16[32,56,128]{2,1,0:T(8,128)(2,1)S(1)}, u32[]{:S(2)}, u32[]{:S(2)}) %all-to-all-start.4) | async-done | bytes 458784 | tf_op jit(solution)/shard_map/all_to_all | solution.py:270
  157.9 0.8 copy-done.2
  158.7 1.9 %unpack.1 = (f32[64,1728]{1,0:T(8,128)}, f32[512,128]{1,0:T(8,128)}, f32[8,3456]{1,0:T(8,128)}) custom-call(bf16[32,56,128]{2,1,0:T(8,128)(2,1)} %copy-done.2), custom_call_target="tpu_custom_call" | custom-call | flops 250000000 | bytes 1048576 | tf_op jit(solution)/shard_map/unpack/pallas_call | solution.py:248
  (30 shorter events, 0.8 us)
Async XLA Ops:
  3.3 10.3 %copy-start.5 = (bf16[1,2,16,1024]{3,2,1,0:T(8,128)(2,1)S(1)}, bf16[1,2,16,1024]{3,2,1,0:T(8,128)(2,1)}, u32[]{:S(2)}) copy-start(bf16[1,2,16,1024]{3,2,1,0:T(8,128)(2,1)} %param.5) | copy-start | bytes 196612
  3.3 34.8 %all-to-all-start = ((bf16[16,8,3584]{2,1,0:T(8,128)(2,1)}), bf16[16,8,3584]{2,1,0:T(8,128)(2,1)S(1)}, u32[]{:S(2)}, u32[]{:S(2)}) async-start(bf16[16,8,3584]{2,1,0:T(8,128)(2,1)} %fusion.1), calls=%async_computation | async-start | bytes 1835008 | tf_op jit(solution)/shard_map/all_to_all | solution.py:270
  13.6 7.7 %collective-permute-start.1 = (bf16[16,1024]{1,0:T(8,128)(2,1)S(1)}, bf16[16,1024]{1,0:T(8,128)(2,1)S(1)}, u32[]{:S(2)}, u32[]{:S(2)}) collective-permute-start(bf16[16,1024]{1,0:T(8,128)(2,1)S(1)} %get-tuple-element.48), channel_id=1, source_target_pairs={{16,0},{32,16},{48,32},{64,48},{80,64},{96,80},{112,96},{128,112},... | collective-permute-start | bytes 98312 | tf_op jit(solution)/shard_map/ppermute | solution.py:266
  16.5 4.8 %collective-permute-start = (bf16[16,1024]{1,0:T(8,128)(2,1)S(1)}, bf16[16,1024]{1,0:T(8,128)(2,1)S(1)}, u32[]{:S(2)}, u32[]{:S(2)}) collective-permute-start(bf16[16,1024]{1,0:T(8,128)(2,1)S(1)} %get-tuple-element.49), channel_id=1, source_target_pairs={{0,16},{16,32},{32,48},{48,64},{64,80},{80,96},{96,112},{112,128},... | collective-permute-start | bytes 98312 | tf_op jit(solution)/shard_map/ppermute | solution.py:266
  21.3 0.6 copy-start.9
  21.3 0.6 copy-start.10
  24.4 5.6 %collective-permute-start.3 = (bf16[64,128]{1,0:T(8,128)(2,1)}, bf16[64,128]{1,0:T(8,128)(2,1)S(1)}, u32[]{:S(2)}, u32[]{:S(2)}) collective-permute-start(bf16[64,128]{1,0:T(8,128)(2,1)} %get-tuple-element.24.own), channel_id=1, source_target_pairs={{16,0},{32,16},{48,32},{64,48},{80,64},{96,80},{112,96},{128,112},... | collective-permute-start | bytes 49160 | tf_op jit(solution)/shard_map/ppermute | solution.py:266
  26.3 4.7 %collective-permute-start.2 = (bf16[64,128]{1,0:T(8,128)(2,1)}, bf16[64,128]{1,0:T(8,128)(2,1)S(1)}, u32[]{:S(2)}, u32[]{:S(2)}) collective-permute-start(bf16[64,128]{1,0:T(8,128)(2,1)} %get-tuple-element.24.own), channel_id=1, source_target_pairs={{0,16},{16,32},{32,48},{48,64},{64,80},{80,96},{96,112},{112,128},... | collective-permute-start | bytes 49160 | tf_op jit(solution)/shard_map/ppermute | solution.py:266
  30.0 8.1 %copy-start.3 = (bf16[64,128]{1,0:T(8,128)(2,1)}, bf16[64,128]{1,0:T(8,128)(2,1)S(1)}, u32[]{:S(2)}) copy-start(bf16[64,128]{1,0:T(8,128)(2,1)S(1)} %collective-permute-done.3.after) | copy-start | bytes 49156
  31.0 7.1 %copy-start.4 = (bf16[64,128]{1,0:T(8,128)(2,1)}, bf16[64,128]{1,0:T(8,128)(2,1)S(1)}, u32[]{:S(2)}) copy-start(bf16[64,128]{1,0:T(8,128)(2,1)S(1)} %collective-permute-done.2.before) | copy-start | bytes 49156
  38.1 0.9 copy-start
  41.5 10.0 %collective-permute-start.5 = (bf16[64,128]{1,0:T(8,128)(2,1)}, bf16[64,128]{1,0:T(8,128)(2,1)S(1)}, u32[]{:S(2)}, u32[]{:S(2)}) collective-permute-start(bf16[64,128]{1,0:T(8,128)(2,1)} %get-tuple-element.25.grad.own), channel_id=1, source_target_pairs={{16,0},{32,16},{48,32},{64,48},{80,64},{96,80},{112,96},{128,112},... | collective-permute-start | bytes 49160 | tf_op jit(solution)/shard_map/ppermute | solution.py:266
  47.2 4.3 %collective-permute-start.4 = (bf16[64,128]{1,0:T(8,128)(2,1)}, bf16[64,128]{1,0:T(8,128)(2,1)S(1)}, u32[]{:S(2)}, u32[]{:S(2)}) collective-permute-start(bf16[64,128]{1,0:T(8,128)(2,1)} %get-tuple-element.25.grad.own), channel_id=1, source_target_pairs={{0,16},{16,32},{32,48},{48,64},{64,80},{80,96},{96,112},{112,128},... | collective-permute-start | bytes 49160 | tf_op jit(solution)/shard_map/ppermute | solution.py:266
  51.5 0.6 copy-start.7
  51.5 0.6 copy-start.8
  52.1 30.4 %copy-start.1 = (bf16[32,128,128]{2,1,0:T(8,128)(2,1)S(1)}, bf16[32,128,128]{2,1,0:T(8,128)(2,1)}, u32[]{:S(2)}) copy-start(bf16[32,128,128]{2,1,0:T(8,128)(2,1)} %coarse_kernel_terms.1) | copy-start | bytes 3145732
  133.4 9.4 %copy-start.6 = (bf16[2,128,128]{2,1,0:T(8,128)(2,1)S(1)}, bf16[2,128,128]{2,1,0:T(8,128)(2,1)}, u32[]{:S(2)}) copy-start(bf16[2,128,128]{2,1,0:T(8,128)(2,1)} %get-tuple-element.35.grad) | copy-start | bytes 196612
  135.2 22.7 %all-to-all-start.4 = ((bf16[32,56,128]{2,1,0:T(8,128)(2,1)}), bf16[32,56,128]{2,1,0:T(8,128)(2,1)S(1)}, u32[]{:S(2)}, u32[]{:S(2)}) async-start(bf16[32,56,128]{2,1,0:T(8,128)(2,1)} %get-tuple-element.37), calls=%async_computation.4 | async-start | bytes 917504 | tf_op jit(solution)/shard_map/all_to_all | solution.py:270
  142.8 5.7 %collective-permute-start.7 = (bf16[128,128]{1,0:T(8,128)(2,1)S(1)}, bf16[128,128]{1,0:T(8,128)(2,1)S(1)}, u32[]{:S(2)}, u32[]{:S(2)}) collective-permute-start(bf16[128,128]{1,0:T(8,128)(2,1)S(1)} %get-tuple-element.46), channel_id=1, source_target_pairs={{16,0},{32,16},{48,32},{64,48},{80,64},{96,80},{112,96},{128,112},... | collective-permute-start | bytes 98312 | tf_op jit(solution)/shard_map/ppermute | solution.py:266
  145.0 4.5 %collective-permute-start.6 = (bf16[128,128]{1,0:T(8,128)(2,1)S(1)}, bf16[128,128]{1,0:T(8,128)(2,1)S(1)}, u32[]{:S(2)}, u32[]{:S(2)}) collective-permute-start(bf16[128,128]{1,0:T(8,128)(2,1)S(1)} %get-tuple-element.47), channel_id=1, source_target_pairs={{0,16},{16,32},{32,48},{48,64},{64,80},{80,96},{96,112},{112,128},... | collective-permute-start | bytes 98312 | tf_op jit(solution)/shard_map/ppermute | solution.py:266
  148.6 1.0 copy-start.11
  149.5 0.6 copy-start.12
  157.9 0.8 copy-start.2

commit v3 on v2

--- a/solution.py
+++ b/solution.py
@@ -120,25 +120,47 @@
     slopes, silu = slope_and_silu(pre)
     scratch[0:64] = silu
     by_x = [scratch[pl.ds(x, 8, stride=8), :] for x in range(8)]
-    ordered = jnp.concatenate(by_x + [jnp.zeros((64, 128), F32)], axis=0)
-    out[...] = ordered.T.astype(BF16)
     scratch[...] = packed[:, 3456:3584].astype(F32).T
     cotangent = jnp.concatenate([scratch[pl.ds(y, 8, stride=8), :] for y in range(8)], axis=0)
-    grad[...] = (cotangent * slopes).astype(BF16)
-
-
-def coarse_kernel_terms(own, before, after, grad, terms):
-    value = grad[...].astype(F32)
-    moved = [shift_rows(value, -1, 8), value, shift_rows(value, 1, 8)]
-    moved = jnp.concatenate(moved, axis=1).astype(BF16)
-    for dz, plane in enumerate((before, own, after)):
-        block = mm(moved, y_taps(plane), TN)
-        for dx in range(3):
-            for dy in range(3):
-                part = block[dx * 128 : (dx + 1) * 128, dy * 128 : (dy + 1) * 128]
-                terms[(dz * 3 + dx) * 3 + dy] = part.astype(BF16)
+    slopes = (cotangent * slopes).astype(BF16)
+    grad[...] = slopes
+    out[...] = jnp.concatenate(by_x + [slopes.astype(F32)], axis=0).T.astype(BF16)
+
+
+def assemble(own, features, before, after, out):
+    sides = jnp.concatenate([before[...].astype(F32), after[...].astype(F32)], axis=0).T
+    for at in range(16):
+        rows = slice(at * 8, at * 8 + 8)
+        out[at, 0:64] = own[...]
+        mixed = jnp.concatenate([features[rows].astype(F32), sides[rows]], axis=0)
+        out[at, 64:80] = mixed.astype(BF16)
+
+
+def coarse_kernel_terms(parts, features, terms, grads, taps):
+    low = low_half(8)
+    place = lax.broadcasted_iota(jnp.int32, (8, 128), 1) % 8
+    for volume in range(16):
+        taps[volume * 64 : (volume + 1) * 64] = y_taps(parts[volume, 0:64])
+        features[volume] = parts[volume, 64:72, 0:64]
+    for pair in range(8):
+        first = parts[pair * 2, 64:80].astype(F32)
+        second = parts[pair * 2 + 1, 64:80].astype(F32)
+        own = jnp.where(low, pltpu.roll(first[0:8], 64, 1), second[0:8])
+        before = jnp.where(low, first[8:16], pltpu.roll(second[8:16], 64, 1))
+        after = jnp.where(low, pltpu.roll(first[8:16], 64, 1), second[8:16])
+        for dz, value in enumerate((after, own, before)):
+            earlier = jnp.where(place != 7, pltpu.roll(value, 127, 1), 0.0)
+            later = jnp.where(place != 0, pltpu.roll(value, 1, 1), 0.0)
+            for dx, moved in enumerate((earlier, value, later)):
+                at = (dz * 3 + dx) * 8
+                grads[at : at + 8, pair * 128 : (pair + 1) * 128] = moved
+    total = mm(grads[...].astype(BF16), taps[...], NN)
+    for k in range(9):
+        for dy in range(3):
+            part = total[k * 8 : k * 8 + 8, dy * 128 : (dy + 1) * 128]
+            terms[k * 3 + dy] = part.astype(BF16)
     for spare in range(27, 32):
-        terms[spare] = jnp.zeros((128, 128), BF16)
+        terms[spare] = jnp.zeros((8, 128), BF16)
 
 
 def backward(own, before, after, packed, pooled, slope, windows, down, shared, fine_grad, act):
@@ -203,35 +225,24 @@
             out[z, :, j * 128 : (j + 1) * 128] = total[at : at + 16]
 
 
-def sum_slabs(terms, shared, features, out):
-    def total(ref, at):
-        return jnp.sum(ref[:, at : at + 16, :].astype(F32), axis=0)
-
-    for pair in range(8):
-        both = total(terms, pair * 16)
-        for half in range(2):
-            at = pair * 2 + half
-            rows = [both[half * 8 : half * 8 + 8], features[at * 8 : at * 8 + 8].astype(F32)]
-            out[at, 0:16] = jnp.concatenate(rows, axis=0).astype(BF16)
-    for part in range(3):
-        rows = total(shared, part * 16).astype(BF16)
-        for at in range(16):
-            out[at, 16 + part * 16 : 32 + part * 16] = rows
-
-
-def sum_groups(parts, features, out):
-    mixed = parts[:, 0:16, :].astype(F32)
-    own = jnp.sum(mixed[:, 0:8], axis=0).astype(BF16)
-    for at in range(16):
-        features[at] = mixed[at, 8:16, 0:64].astype(BF16)
-    rows = [
-        jnp.sum(parts[:, 16 + part * 16 : 32 + part * 16, :].astype(F32), axis=0).astype(BF16)
-        for part in range(3)
-    ]
-    for at in range(32):
+def sum_of(parts, at):
+    return jnp.sum(parts[:, at : at + 16, :].astype(F32), axis=0).astype(BF16)
+
+
+def sum_slabs(shared, out):
+    for at in range(0, 48, 16):
+        rows = sum_of(shared, at)
+        for device in range(16):
+            out[device, at : at + 16] = rows
+
+
+def sum_groups(shared, terms, out):
+    own = jnp.sum(terms[...].astype(F32), axis=0).astype(BF16)
+    rows = [sum_of(shared, at) for at in range(0, 48, 16)]
+    for device in range(32):
         for part in range(3):
-            out[at, part * 16 : part * 16 + 16] = rows[part]
-        out[at, 48:56] = own
+            out[device, part * 16 : part * 16 + 16] = rows[part]
+        out[device, 48:56] = own
 
 
 def unpack(parts, fine, down, coarse):
@@ -244,15 +255,16 @@
         coarse[:, tap * 128 : (tap + 1) * 128] = parts[tap, 48:56, :].astype(F32)
 
 
-def call(body, name, outs, *operands, scratch=()):
+def call(body, name, outs, *operands, scratch=(), final=0):
+    place = [jax.ShapeDtypeStruct] * final + [pltpu.VMEM] * (len(outs) - final)
     return pl.pallas_call(
         body,
-        out_shape=[jax.ShapeDtypeStruct(shape, kind) for shape, kind in outs],
+        out_shape=[put(*out) for put, out in zip(place, outs)],
         scratch_shapes=[pltpu.VMEM(shape, kind) for shape, kind in scratch],
         name=name,
         cost_estimate=pl.CostEstimate(flops=WORK, transcendentals=0, bytes_accessed=1 << 20),
         interpret=INTERPRET,
-    )(*operands)
+    )(*[pltpu.with_memory_space_constraint(operand, pltpu.VMEM) for operand in operands])
 
 
 INTERPRET = False
@@ -301,14 +313,13 @@
         scratch=[((128, 128), F32)],
     )
     grad_before, grad_after = from_sides(coarse_grad, coarse_grad)
-    (terms,) = call(
-        coarse_kernel_terms,
-        "coarse_kernel_terms",
-        [((slabs, 128, 128), BF16)],
-        coarse_in, in_before, in_after, coarse_grad,
-    )
-    grad_before, grad_after, terms = lax.optimization_barrier((grad_before, grad_after, terms))
-    terms = exchange(terms, "gz")
+    (parts,) = call(
+        assemble,
+        "assemble",
+        [((group, 80, 128), BF16)],
+        coarse_in, features, grad_before, grad_after,
+    )
+    parts = exchange(parts, "grp")
     shared, fine_grad = call(
         backward,
         "backward",
@@ -317,6 +328,15 @@
         scratch=[((256, 128), F32)],
     )
     shared = exchange(shared.reshape(slabs, 48, 128), "gz")
+    out_rows, terms = call(
+        coarse_kernel_terms,
+        "coarse_kernel_terms",
+        [((group, 8, 64), BF16), ((slabs, 8, 128), BF16)],
+        parts,
+        scratch=[((72, 1024), F32), ((1024, 384), BF16)],
+        final=1,
+    )
+    terms = exchange(terms, "gz")
     fine_before, fine_after = from_sides(fine_grad[1], fine_grad[0])
     (volume_grad,) = call(
         fine_backward,
@@ -324,15 +344,18 @@
         [((2, 16, 1024), BF16)],
         fine_grad, fine_before, fine_after, behind,
         scratch=[((4, 128, 256), BF16)],
-    )
-    (parts,) = call(sum_slabs, "sum_slabs", [((group, 64, 128), BF16)], terms, shared, features)
-    parts = exchange(parts, "grp")
-    out_rows, final = call(
-        sum_groups, "sum_groups", [((group, 8, 64), BF16), ((slabs, 56, 128), BF16)], parts
-    )
+        final=1,
+    )
+    (shared,) = call(sum_slabs, "sum_slabs", [((group, 48, 128), BF16)], shared)
+    shared = exchange(shared, "grp")
+    (final,) = call(sum_groups, "sum_groups", [((slabs, 56, 128), BF16)], shared, terms)
     final = exchange(final, "gz")
     fine_kg, down_kg, coarse_kg = call(
-        unpack, "unpack", [((64, 1728), F32), ((512, 128), F32), ((8, 3456), F32)], final
+        unpack,
+        "unpack",
+        [((64, 1728), F32), ((512, 128), F32), ((8, 3456), F32)],
+        final,
+        final=3,
     )
     coarse_out = jnp.swapaxes(out_rows, 1, 2)[:, None]
     return (coarse_out, volume_grad[None], fine_kg.T, down_kg, coarse_kg.T)

time: 162 us -> 145 us (0.90)
  blocking collectives: 75.9 us -> 14 us
  waiting for transfers between devices: 14.7 us -> 52.7 us
  starting transfers between devices: 42.5 us -> 63.6 us
  Pallas kernels: 20.5 us -> 7.83 us
    all_to_all x3 -> x1, blocking collectives: 75.9 us -> 14 us  [exchange(): return lax.all_to_all(blocks, axis, 0, 0, tiled=True)]
    all_to_all x2 -> x5, waiting for transfers between devices: 12.6 us -> 49.6 us  [exchange(): return lax.all_to_all(blocks, axis, 0, 0, tiled=True)]
    all_to_all x2 -> x5, starting transfers between devices: 17.9 us -> 39 us  [exchange(): return lax.all_to_all(blocks, axis, 0, 0, tiled=True)]
    pallas_call x9 -> x10, Pallas kernels: 20.5 us -> 7.83 us  [call(): pl.pallas_call(body, out_shape=[put(*out) for put, out in zip(place, outs...]
    unnamed x26 -> x16, local copies, waits for them, and re-layouts: 3.52 us -> 2.73 us
  transfers between devices with their start and end apart: 10 -> 13, of which waited for: 5 -> 9; matrix products, arithmetic and copies ran while one was open for 0% -> 0% of each run, Pallas kernels for 6% -> 3%
where the time goes in v3:
time: 145 us; the launch traced here: 144 us
  starting transfers between devices  63.6 us (44%)
  waiting for transfers between devices  52.7 us (36%)
  blocking collectives  14 us (10%)
  Pallas kernels  7.83 us (5%)
  local copies, waits for them, and re-layouts  3.62 us (2%)
    all_to_all x5, waiting for transfers between devices, exchange(): return lax.all_to_all(blocks, axis, 0, 0, tiled=True)  49.6 us
    all_to_all x5, starting transfers between devices, exchange(): return lax.all_to_all(blocks, axis, 0, 0, tiled=True)  39 us
    ppermute x8, starting transfers between devices, from_sides(): return (lax.ppermute(last, 'gz', up), lax.ppermute(first, 'gz', down))  24.6 us
    all_to_all x1, blocking collectives, exchange(): return lax.all_to_all(blocks, axis, 0, 0, tiled=True)  14 us
    pallas_call x10, Pallas kernels, call(): pl.pallas_call(body, out_shape=[put(*out) for put, out in zip(place, outs...  7.83 us
    ppermute x8, waiting for transfers between devices, from_sides(): return (lax.ppermute(last, 'gz', up), lax.ppermute(first, 'gz', down))  3.15 us
  transfers between devices with their start and end apart: 13, of which 9 were waited for; matrix products, arithmetic and copies ran while one was open for 0% of the time, Pallas kernels for 3%

profile of v3, /device:TPU:1, one launch (start us, length us, event | category | flops | bytes accessed | tf_op | source)
XLA Modules:
  0.0 143.6 jit_solution(13553147987665837226)
XLA Ops:
  0.6 0.9 broadcast_in_dim.12
  1.5 1.0 fusion.1
  2.5 10.3 %all-to-all-start = ((bf16[16,8,3584]{2,1,0:T(8,128)(2,1)}), bf16[16,8,3584]{2,1,0:T(8,128)(2,1)S(1)}, u32[]{:S(2)}, u32[]{:S(2)}) async-start(bf16[16,8,3584]{2,1,0:T(8,128)(2,1)} %fusion.1), calls=%async_computation | async-start | bytes 1835008 | tf_op jit(solution)/shard_map/all_to_all | solution.py:282
  12.9 3.0 %collective-permute-start.1 = (bf16[16,1024]{1,0:T(8,128)(2,1)S(1)}, bf16[16,1024]{1,0:T(8,128)(2,1)S(1)}, u32[]{:S(2)}, u32[]{:S(2)}) collective-permute-start(bf16[16,1024]{1,0:T(8,128)(2,1)S(1)} %get-tuple-element.42), channel_id=1, source_target_pairs={{16,0},{32,16},{48,32},{64,48},{80,64},{96,80},{112,96},{128,112},... | collective-permute-start | bytes 98312 | tf_op jit(solution)/shard_map/ppermute | solution.py:278
  15.9 2.7 %collective-permute-start = (bf16[16,1024]{1,0:T(8,128)(2,1)S(1)}, bf16[16,1024]{1,0:T(8,128)(2,1)S(1)}, u32[]{:S(2)}, u32[]{:S(2)}) collective-permute-start(bf16[16,1024]{1,0:T(8,128)(2,1)S(1)} %get-tuple-element.43), channel_id=1, source_target_pairs={{0,16},{16,32},{32,48},{48,64},{64,80},{80,96},{96,112},{112,128},... | collective-permute-start | bytes 98312 | tf_op jit(solution)/shard_map/ppermute | solution.py:278
  19.6 0.8 copy-done.5
  20.5 1.1 copy-done.4
  22.2 1.9 %collective-permute-start.3 = (bf16[64,128]{1,0:T(8,128)(2,1)S(1)}, bf16[64,128]{1,0:T(8,128)(2,1)S(1)}, u32[]{:S(2)}, u32[]{:S(2)}) collective-permute-start(bf16[64,128]{1,0:T(8,128)(2,1)S(1)} %get-tuple-element.21.own), channel_id=1, source_target_pairs={{16,0},{32,16},{48,32},{64,48},{80,64},{96,80},{112,96},{128,112},... | collective-permute-start | bytes 49160 | tf_op jit(solution)/shard_map/ppermute | solution.py:278
  24.1 3.6 %collective-permute-start.2 = (bf16[64,128]{1,0:T(8,128)(2,1)S(1)}, bf16[64,128]{1,0:T(8,128)(2,1)S(1)}, u32[]{:S(2)}, u32[]{:S(2)}) collective-permute-start(bf16[64,128]{1,0:T(8,128)(2,1)S(1)} %get-tuple-element.21.own), channel_id=1, source_target_pairs={{0,16},{16,32},{32,48},{48,64},{64,80},{80,96},{96,112},{112,128},... | collective-permute-start | bytes 49160 | tf_op jit(solution)/shard_map/ppermute | solution.py:278
  27.8 1.2 collective-permute-done.3.after
  29.0 8.5 %all-to-all-done = bf16[16,8,3584]{2,1,0:T(8,128)(2,1)S(1)} async-done(((bf16[16,8,3584]{2,1,0:T(8,128)(2,1)}), bf16[16,8,3584]{2,1,0:T(8,128)(2,1)S(1)}, u32[]{:S(2)}, u32[]{:S(2)}) %all-to-all-start) | async-done | bytes 917536 | tf_op jit(solution)/shard_map/all_to_all | solution.py:282
  38.0 5.7 %collective-permute-start.5 = (bf16[64,128]{1,0:T(8,128)(2,1)S(1)}, bf16[64,128]{1,0:T(8,128)(2,1)S(1)}, u32[]{:S(2)}, u32[]{:S(2)}) collective-permute-start(bf16[64,128]{1,0:T(8,128)(2,1)S(1)} %get-tuple-element.23.own), channel_id=1, source_target_pairs={{16,0},{32,16},{48,32},{64,48},{80,64},{96,80},{112,96},{128,112},... | collective-permute-start | bytes 49160 | tf_op jit(solution)/shard_map/ppermute | solution.py:278
  43.7 2.1 %collective-permute-start.4 = (bf16[64,128]{1,0:T(8,128)(2,1)S(1)}, bf16[64,128]{1,0:T(8,128)(2,1)S(1)}, u32[]{:S(2)}, u32[]{:S(2)}) collective-permute-start(bf16[64,128]{1,0:T(8,128)(2,1)S(1)} %get-tuple-element.23.own), channel_id=1, source_target_pairs={{0,16},{16,32},{32,48},{48,64},{64,80},{80,96},{96,112},{112,128},... | collective-permute-start | bytes 49160 | tf_op jit(solution)/shard_map/ppermute | solution.py:278
  45.8 1.0 collective-permute-done.4.before
  46.8 0.8 assemble.1
  47.6 3.5 %all-to-all-start.1 = ((bf16[16,80,128]{2,1,0:T(8,128)(2,1)}), bf16[16,80,128]{2,1,0:T(8,128)(2,1)S(1)}, u32[]{:S(2)}, u32[]{:S(2)}) async-start(bf16[16,80,128]{2,1,0:T(8,128)(2,1)} %assemble.1), calls=%async_computation.1 | async-start | bytes 655360 | tf_op jit(solution)/shard_map/all_to_all | solution.py:282
  51.2 1.6 %backward.1 = (bf16[1536,128]{1,0:T(8,128)(2,1)}, bf16[2,128,128]{2,1,0:T(8,128)(2,1)S(1)}) custom-call(bf16[64,128]{1,0:T(8,128)(2,1)S(1)} %get-tuple-element.23.own, bf16[64,128]{1,0:T(8,128)(2,1)S(1)} %collective-permute-done.4.before, bf16[64,128]{1,0:T(8,128)(2,1)S(1)} %collective-permute-done.5.after, bf16[128,3584]{1,0:T(8,128)(2,1)S(1)} %bitcast.25, ...), custom_call_target="tpu_custom_call" | custom-call | flops 250000000 | bytes 1048576 | tf_op jit(solution)/shard_map/backward/pallas_call | solution.py:260
  52.8 12.6 %all-to-all-done.1.parts = bf16[16,80,128]{2,1,0:T(8,128)(2,1)S(1)} async-done(((bf16[16,80,128]{2,1,0:T(8,128)(2,1)}), bf16[16,80,128]{2,1,0:T(8,128)(2,1)S(1)}, u32[]{:S(2)}, u32[]{:S(2)}) %all-to-all-start.1) | async-done | bytes 327712 | tf_op jit(solution)/shard_map/all_to_all | solution.py:282
  65.4 14.2 %all-to-all-start.2 = ((bf16[32,48,128]{2,1,0:T(8,128)(2,1)}), bf16[32,48,128]{2,1,0:T(8,128)(2,1)S(1)}, u32[]{:S(2)}, u32[]{:S(2)}) async-start(bf16[32,48,128]{2,1,0:T(8,128)(2,1)} %bitcast.14), calls=%async_computation.2 | async-start | bytes 786432 | tf_op jit(solution)/shard_map/all_to_all | solution.py:282
  79.6 1.0 coarse_kernel_terms.1
  80.6 12.7 %all-to-all-done.2.shared = bf16[32,48,128]{2,1,0:T(8,128)(2,1)S(1)} async-done(((bf16[32,48,128]{2,1,0:T(8,128)(2,1)}), bf16[32,48,128]{2,1,0:T(8,128)(2,1)S(1)}, u32[]{:S(2)}, u32[]{:S(2)}) %all-to-all-start.2) | async-done | bytes 393248 | tf_op jit(solution)/shard_map/all_to_all | solution.py:282
  93.3 5.2 %all-to-all-start.4 = ((bf16[32,8,128]{2,1,0:T(8,128)(2,1)}), bf16[32,8,128]{2,1,0:T(8,128)(2,1)S(1)}, u32[]{:S(2)}, u32[]{:S(2)}) async-start(bf16[32,8,128]{2,1,0:T(8,128)(2,1)} %get-tuple-element.31), calls=%async_computation.4 | async-start | bytes 131072 | tf_op jit(solution)/shard_map/all_to_all | solution.py:282
  98.6 8.3 %all-to-all-done.4.terms = bf16[32,8,128]{2,1,0:T(8,128)(2,1)S(1)} async-done(((bf16[32,8,128]{2,1,0:T(8,128)(2,1)}), bf16[32,8,128]{2,1,0:T(8,128)(2,1)S(1)}, u32[]{:S(2)}, u32[]{:S(2)}) %all-to-all-start.4) | async-done | bytes 65568 | tf_op jit(solution)/shard_map/all_to_all | solution.py:282
  106.9 14.0 %all_to_all.30.shared = bf16[16,48,128]{2,1,0:T(8,128)(2,1)S(1)} all-to-all(bf16[16,48,128]{2,1,0:T(8,128)(2,1)S(1)} %sum_slabs.1), channel_id=1, replica_groups=mesh['gz'=32,'grp'=16] {'grp'}, dimensions={0} | all-to-all | bytes 393216 | tf_op jit(solution)/shard_map/all_to_all | solution.py:282
  120.9 0.8 sum_groups.1
  121.7 5.7 %all-to-all-start.5 = ((bf16[32,56,128]{2,1,0:T(8,128)(2,1)}), bf16[32,56,128]{2,1,0:T(8,128)(2,1)S(1)}, u32[]{:S(2)}, u32[]{:S(2)}) async-start(bf16[32,56,128]{2,1,0:T(8,128)(2,1)} %sum_groups.1), calls=%async_computation.5 | async-start | bytes 917504 | tf_op jit(solution)/shard_map/all_to_all | solution.py:282
  127.5 2.3 %collective-permute-start.7 = (bf16[128,128]{1,0:T(8,128)(2,1)S(1)}, bf16[128,128]{1,0:T(8,128)(2,1)S(1)}, u32[]{:S(2)}, u32[]{:S(2)}) collective-permute-start(bf16[128,128]{1,0:T(8,128)(2,1)S(1)} %get-tuple-element.40), channel_id=1, source_target_pairs={{16,0},{32,16},{48,32},{64,48},{80,64},{96,80},{112,96},{128,112},... | collective-permute-start | bytes 98312 | tf_op jit(solution)/shard_map/ppermute | solution.py:278
  129.7 3.3 %collective-permute-start.6 = (bf16[128,128]{1,0:T(8,128)(2,1)S(1)}, bf16[128,128]{1,0:T(8,128)(2,1)S(1)}, u32[]{:S(2)}, u32[]{:S(2)}) collective-permute-start(bf16[128,128]{1,0:T(8,128)(2,1)S(1)} %get-tuple-element.41), channel_id=1, source_target_pairs={{0,16},{16,32},{32,48},{48,64},{64,80},{80,96},{96,112},{112,128},... | collective-permute-start | bytes 98312 | tf_op jit(solution)/shard_map/ppermute | solution.py:278
  133.2 0.8 collective-permute-done.6.before
  134.0 1.1 fine_backward.1
  135.1 7.5 %all-to-all-done.5.parts = bf16[32,56,128]{2,1,0:T(8,128)(2,1)S(1)} async-done(((bf16[32,56,128]{2,1,0:T(8,128)(2,1)}), bf16[32,56,128]{2,1,0:T(8,128)(2,1)S(1)}, u32[]{:S(2)}, u32[]{:S(2)}) %all-to-all-start.5) | async-done | bytes 458784 | tf_op jit(solution)/shard_map/all_to_all | solution.py:282
  142.7 0.9 unpack.1
  (25 shorter events, 2.5 us)
Async XLA Ops:
  0.6 0.9 copy-start.7
  2.5 10.3 %copy-start.1 = (bf16[1,2,16,1024]{3,2,1,0:T(8,128)(2,1)S(1)}, bf16[1,2,16,1024]{3,2,1,0:T(8,128)(2,1)}, u32[]{:S(2)}) copy-start(bf16[1,2,16,1024]{3,2,1,0:T(8,128)(2,1)} %param.5) | copy-start | bytes 196612
  2.5 16.1 %copy-start.2 = (bf16[1728,64]{0,1:T(8,128)(2,1)S(1)}, bf16[1728,64]{0,1:T(8,128)(2,1)}, u32[]{:S(2)}) copy-start(bf16[1728,64]{0,1:T(8,128)(2,1)} %param.7) | copy-start | bytes 663556
  2.5 34.9 %all-to-all-start = ((bf16[16,8,3584]{2,1,0:T(8,128)(2,1)}), bf16[16,8,3584]{2,1,0:T(8,128)(2,1)S(1)}, u32[]{:S(2)}, u32[]{:S(2)}) async-start(bf16[16,8,3584]{2,1,0:T(8,128)(2,1)} %fusion.1), calls=%async_computation | async-start | bytes 1835008 | tf_op jit(solution)/shard_map/all_to_all | solution.py:282
  12.9 7.6 %copy-start = (bf16[512,128]{1,0:T(8,128)(2,1)S(1)}, bf16[512,128]{1,0:T(8,128)(2,1)}, u32[]{:S(2)}) copy-start(bf16[512,128]{1,0:T(8,128)(2,1)} %down.3) | copy-start | bytes 393220
  12.9 7.5 %collective-permute-start.1 = (bf16[16,1024]{1,0:T(8,128)(2,1)S(1)}, bf16[16,1024]{1,0:T(8,128)(2,1)S(1)}, u32[]{:S(2)}, u32[]{:S(2)}) collective-permute-start(bf16[16,1024]{1,0:T(8,128)(2,1)S(1)} %get-tuple-element.42), channel_id=1, source_target_pairs={{16,0},{32,16},{48,32},{64,48},{80,64},{96,80},{112,96},{128,112},... | collective-permute-start | bytes 98312 | tf_op jit(solution)/shard_map/ppermute | solution.py:278
  15.9 4.5 %collective-permute-start = (bf16[16,1024]{1,0:T(8,128)(2,1)S(1)}, bf16[16,1024]{1,0:T(8,128)(2,1)S(1)}, u32[]{:S(2)}, u32[]{:S(2)}) collective-permute-start(bf16[16,1024]{1,0:T(8,128)(2,1)S(1)} %get-tuple-element.43), channel_id=1, source_target_pairs={{0,16},{16,32},{32,48},{48,64},{64,80},{80,96},{96,112},{112,128},... | collective-permute-start | bytes 98312 | tf_op jit(solution)/shard_map/ppermute | solution.py:278
  18.8 0.8 copy-start.3
  19.6 0.8 copy-start.5
  20.5 1.1 copy-start.4
  22.2 6.8 %collective-permute-start.3 = (bf16[64,128]{1,0:T(8,128)(2,1)S(1)}, bf16[64,128]{1,0:T(8,128)(2,1)S(1)}, u32[]{:S(2)}, u32[]{:S(2)}) collective-permute-start(bf16[64,128]{1,0:T(8,128)(2,1)S(1)} %get-tuple-element.21.own), channel_id=1, source_target_pairs={{16,0},{32,16},{48,32},{64,48},{80,64},{96,80},{112,96},{128,112},... | collective-permute-start | bytes 49160 | tf_op jit(solution)/shard_map/ppermute | solution.py:278
  24.1 4.8 %collective-permute-start.2 = (bf16[64,128]{1,0:T(8,128)(2,1)S(1)}, bf16[64,128]{1,0:T(8,128)(2,1)S(1)}, u32[]{:S(2)}, u32[]{:S(2)}) collective-permute-start(bf16[64,128]{1,0:T(8,128)(2,1)S(1)} %get-tuple-element.21.own), channel_id=1, source_target_pairs={{0,16},{16,32},{32,48},{48,64},{64,80},{80,96},{96,112},{112,128},... | collective-permute-start | bytes 49160 | tf_op jit(solution)/shard_map/ppermute | solution.py:278
  38.0 7.8 %collective-permute-start.5 = (bf16[64,128]{1,0:T(8,128)(2,1)S(1)}, bf16[64,128]{1,0:T(8,128)(2,1)S(1)}, u32[]{:S(2)}, u32[]{:S(2)}) collective-permute-start(bf16[64,128]{1,0:T(8,128)(2,1)S(1)} %get-tuple-element.23.own), channel_id=1, source_target_pairs={{16,0},{32,16},{48,32},{64,48},{80,64},{96,80},{112,96},{128,112},... | collective-permute-start | bytes 49160 | tf_op jit(solution)/shard_map/ppermute | solution.py:278
  43.7 3.1 %collective-permute-start.4 = (bf16[64,128]{1,0:T(8,128)(2,1)S(1)}, bf16[64,128]{1,0:T(8,128)(2,1)S(1)}, u32[]{:S(2)}, u32[]{:S(2)}) collective-permute-start(bf16[64,128]{1,0:T(8,128)(2,1)S(1)} %get-tuple-element.23.own), channel_id=1, source_target_pairs={{0,16},{16,32},{32,48},{48,64},{64,80},{80,96},{96,112},{112,128},... | collective-permute-start | bytes 49160 | tf_op jit(solution)/shard_map/ppermute | solution.py:278
  47.6 17.7 %all-to-all-start.1 = ((bf16[16,80,128]{2,1,0:T(8,128)(2,1)}), bf16[16,80,128]{2,1,0:T(8,128)(2,1)S(1)}, u32[]{:S(2)}, u32[]{:S(2)}) async-start(bf16[16,80,128]{2,1,0:T(8,128)(2,1)} %assemble.1), calls=%async_computation.1 | async-start | bytes 655360 | tf_op jit(solution)/shard_map/all_to_all | solution.py:282
  65.4 27.9 %all-to-all-start.2 = ((bf16[32,48,128]{2,1,0:T(8,128)(2,1)}), bf16[32,48,128]{2,1,0:T(8,128)(2,1)S(1)}, u32[]{:S(2)}, u32[]{:S(2)}) async-start(bf16[32,48,128]{2,1,0:T(8,128)(2,1)} %bitcast.14), calls=%async_computation.2 | async-start | bytes 786432 | tf_op jit(solution)/shard_map/all_to_all | solution.py:282
  93.3 13.6 %all-to-all-start.4 = ((bf16[32,8,128]{2,1,0:T(8,128)(2,1)}), bf16[32,8,128]{2,1,0:T(8,128)(2,1)S(1)}, u32[]{:S(2)}, u32[]{:S(2)}) async-start(bf16[32,8,128]{2,1,0:T(8,128)(2,1)} %get-tuple-element.31), calls=%async_computation.4 | async-start | bytes 131072 | tf_op jit(solution)/shard_map/all_to_all | solution.py:282
  120.9 13.2 %copy-start.6 = (bf16[9,256,128]{2,1,0:T(8,128)(2,1)S(1)}, bf16[9,256,128]{2,1,0:T(8,128)(2,1)}, u32[]{:S(2)}) copy-start(bf16[9,256,128]{2,1,0:T(8,128)(2,1)} %copy-done.5) | copy-start | bytes 1769476
  121.7 21.0 %all-to-all-start.5 = ((bf16[32,56,128]{2,1,0:T(8,128)(2,1)}), bf16[32,56,128]{2,1,0:T(8,128)(2,1)S(1)}, u32[]{:S(2)}, u32[]{:S(2)}) async-start(bf16[32,56,128]{2,1,0:T(8,128)(2,1)} %sum_groups.1), calls=%async_computation.5 | async-start | bytes 917504 | tf_op jit(solution)/shard_map/all_to_all | solution.py:282
  127.5 5.8 %collective-permute-start.7 = (bf16[128,128]{1,0:T(8,128)(2,1)S(1)}, bf16[128,128]{1,0:T(8,128)(2,1)S(1)}, u32[]{:S(2)}, u32[]{:S(2)}) collective-permute-start(bf16[128,128]{1,0:T(8,128)(2,1)S(1)} %get-tuple-element.40), channel_id=1, source_target_pairs={{16,0},{32,16},{48,32},{64,48},{80,64},{96,80},{112,96},{128,112},... | collective-permute-start | bytes 98312 | tf_op jit(solution)/shard_map/ppermute | solution.py:278
  129.7 4.3 %collective-permute-start.6 = (bf16[128,128]{1,0:T(8,128)(2,1)S(1)}, bf16[128,128]{1,0:T(8,128)(2,1)S(1)}, u32[]{:S(2)}, u32[]{:S(2)}) collective-permute-start(bf16[128,128]{1,0:T(8,128)(2,1)S(1)} %get-tuple-element.41), channel_id=1, source_target_pairs={{0,16},{16,32},{32,48},{48,64},{64,80},{80,96},{96,112},{112,128},... | collective-permute-start | bytes 98312 | tf_op jit(solution)/shard_map/ppermute | solution.py:278

commit v4 on v3

--- a/solution.py
+++ b/solution.py
@@ -106,7 +106,38 @@
     return jnp.concatenate([earlier, value, later], axis=1).astype(BF16)
 
 
-def coarse_forward(own, before, after, packed, grad, out, scratch):
+HALF = 1792
+
+
+def spread_half(core, kernel, cotangent, out):
+    for at in range(16):
+        tail = jnp.concatenate([cotangent[at].astype(F32), jnp.zeros((8, 64), F32)], axis=1)
+        out[at, :, HALF : HALF + 128] = tail.astype(BF16)
+
+    @pl.when(core[0] == 0)
+    def _():
+        for at in range(16):
+            out[at, :, 0:HALF] = kernel[:, 0:HALF]
+
+    @pl.when(core[0] == 1)
+    def _():
+        for at in range(16):
+            out[at, :, 0:HALF] = kernel[:, 3456 - HALF : 3456]
+
+
+def coarse_forward(core, own, before, after, mine, other, grad, out, packed, scratch):
+    rest = 3456 - HALF
+
+    @pl.when(core[0] == 0)
+    def _():
+        packed[:, 0:HALF] = mine[:, 0:HALF]
+        packed[:, HALF:3456] = other[:, HALF - rest : HALF]
+
+    @pl.when(core[0] == 1)
+    def _():
+        packed[:, 0:rest] = other[:, 0:rest]
+        packed[:, rest:3456] = mine[:, 0:HALF]
+
     planes = [y_taps(before), y_taps(own), y_taps(after)]
     parts = []
     for dx in range(3):
@@ -120,20 +151,11 @@
     slopes, silu = slope_and_silu(pre)
     scratch[0:64] = silu
     by_x = [scratch[pl.ds(x, 8, stride=8), :] for x in range(8)]
-    scratch[...] = packed[:, 3456:3584].astype(F32).T
+    scratch[...] = mine[:, HALF : HALF + 128].astype(F32).T
     cotangent = jnp.concatenate([scratch[pl.ds(y, 8, stride=8), :] for y in range(8)], axis=0)
     slopes = (cotangent * slopes).astype(BF16)
     grad[...] = slopes
     out[...] = jnp.concatenate(by_x + [slopes.astype(F32)], axis=0).T.astype(BF16)
-
-
-def assemble(own, features, before, after, out):
-    sides = jnp.concatenate([before[...].astype(F32), after[...].astype(F32)], axis=0).T
-    for at in range(16):
-        rows = slice(at * 8, at * 8 + 8)
-        out[at, 0:64] = own[...]
-        mixed = jnp.concatenate([features[rows].astype(F32), sides[rows]], axis=0)
-        out[at, 64:80] = mixed.astype(BF16)
 
 
 def coarse_kernel_terms(parts, features, terms, grads, taps):
@@ -155,15 +177,22 @@
                 at = (dz * 3 + dx) * 8
                 grads[at : at + 8, pair * 128 : (pair + 1) * 128] = moved
     total = mm(grads[...].astype(BF16), taps[...], NN)
-    for k in range(9):
-        for dy in range(3):
-            part = total[k * 8 : k * 8 + 8, dy * 128 : (dy + 1) * 128]
-            terms[k * 3 + dy] = part.astype(BF16)
-    for spare in range(27, 32):
-        terms[spare] = jnp.zeros((8, 128), BF16)
-
-
-def backward(own, before, after, packed, pooled, slope, windows, down, shared, fine_grad, act):
+    shared = []
+    for at in range(80, 176, 16):
+        both = jnp.sum(parts[:, at : at + 16, :].astype(F32), axis=0)
+        shared += [both[0:8], both[8:16]]
+    none = jnp.zeros((8, 128), F32)
+    for device in range(32):
+        k, dy = divmod(device, 3)
+        own = total[k * 8 : k * 8 + 8, dy * 128 : (dy + 1) * 128] if device < 27 else none
+        other = shared[device] if device < 12 else none
+        terms[device] = jnp.concatenate([own, other], axis=0).astype(BF16)
+
+
+def backward(
+    own, before, after, packed, pooled, slope, windows, down, coarse_in, features,
+    out, fine_grad, act, shared,
+):
     planes = [after[...], own[...], before[...]]
     edge = jnp.zeros((8, 128), F32)
     parts = []
@@ -208,6 +237,13 @@
     shared[832:896] = jnp.where(low, held, 0.0).astype(BF16)
     shared[896:1408] = mm(pooled[...], in_grad, TN).astype(BF16)
     shared[1408:1536] = jnp.zeros((128, 128), BF16)
+    sides = jnp.concatenate([before[...].astype(F32), after[...].astype(F32)], axis=0).T
+    for at in range(16):
+        rows = slice(at * 8, at * 8 + 8)
+        out[at, 0:64] = coarse_in[...]
+        mixed = jnp.concatenate([features[rows].astype(F32), sides[rows]], axis=0)
+        out[at, 64:80] = mixed.astype(BF16)
+        out[at, 80:176] = shared[at * 96 : at * 96 + 96]
 
 
 def fine_backward(grad, before, after, weights, out, windows):
@@ -225,46 +261,47 @@
             out[z, :, j * 128 : (j + 1) * 128] = total[at : at + 16]
 
 
-def sum_of(parts, at):
-    return jnp.sum(parts[:, at : at + 16, :].astype(F32), axis=0).astype(BF16)
-
-
-def sum_slabs(shared, out):
-    for at in range(0, 48, 16):
-        rows = sum_of(shared, at)
+def sum_slabs(terms, out):
+    total = jnp.sum(terms[...].astype(F32), axis=0).astype(BF16)
+    for device in range(32):
+        out[device] = total
+
+
+def collect(terms, coarse, out):
+    rows = []
+    for device in range(27):
+        both = terms[device].astype(F32)
+        coarse[:, device * 128 : (device + 1) * 128] = both[0:8]
+        rows.append(both[8:16])
+    for pair in range(6):
+        both = jnp.concatenate(rows[pair * 2 : pair * 2 + 2], axis=0).astype(BF16)
         for device in range(16):
-            out[device, at : at + 16] = rows
-
-
-def sum_groups(shared, terms, out):
-    own = jnp.sum(terms[...].astype(F32), axis=0).astype(BF16)
-    rows = [sum_of(shared, at) for at in range(0, 48, 16)]
-    for device in range(32):
-        for part in range(3):
-            out[device, part * 16 : part * 16 + 16] = rows[part]
-        out[device, 48:56] = own
-
-
-def unpack(parts, fine, down, coarse):
-    shared = parts[:, 0:48, :].astype(F32).reshape(1536, 128)
+            out[device, pair * 16 : pair * 16 + 16] = both
+
+
+def unpack(shared, fine, down):
     for tile in range(13):
-        fine[:, tile * 128 : (tile + 1) * 128] = shared[tile * 64 : (tile + 1) * 64]
-    fine[:, 1664:1728] = shared[832:896, 0:64]
-    down[...] = shared[896:1408]
-    for tap in range(27):
-        coarse[:, tap * 128 : (tap + 1) * 128] = parts[tap, 48:56, :].astype(F32)
-
-
-def call(body, name, outs, *operands, scratch=(), final=0):
-    place = [jax.ShapeDtypeStruct] * final + [pltpu.VMEM] * (len(outs) - final)
+        rows = shared[tile * 64 : (tile + 1) * 64]
+        fine[:, tile * 128 : (tile + 1) * 128] = rows.astype(F32)
+    fine[:, 1664:1728] = shared[832:896].astype(F32)[:, 0:64]
+    down[...] = shared[896:1408].astype(F32)
+
+
+def call(body, name, outs, *operands, scratch=(), far=(), core=None, moved=True):
+    place = [jax.ShapeDtypeStruct if at in far else pltpu.VMEM for at in range(len(outs))]
+    first = [] if core is None else [core]
+    if moved:
+        operands = [pltpu.with_memory_space_constraint(part, pltpu.VMEM) for part in operands]
+    specs = [pl.BlockSpec(memory_space=pltpu.SMEM) for _ in first]
     return pl.pallas_call(
         body,
         out_shape=[put(*out) for put, out in zip(place, outs)],
+        in_specs=specs + [pl.BlockSpec(memory_space=pltpu.VMEM) for _ in operands],
         scratch_shapes=[pltpu.VMEM(shape, kind) for shape, kind in scratch],
         name=name,
         cost_estimate=pl.CostEstimate(flops=WORK, transcendentals=0, bytes_accessed=1 << 20),
         interpret=INTERPRET,
-    )(*[pltpu.with_memory_space_constraint(operand, pltpu.VMEM) for operand in operands])
+    )(*first, *operands)
 
 
 INTERPRET = False
@@ -287,14 +324,22 @@
     slabs = lax.axis_size("gz")
     vol = volumes[0]
     before, after = from_sides(vol[1], vol[0])
-    kernel_rows = jnp.broadcast_to(coarse_kernel.T[None], (group, 8, 3456))
-    cot_rows = jnp.pad(jnp.swapaxes(cotangent[:, 0], 1, 2), ((0, 0), (0, 0), (0, 64)))
-    packed = exchange(jnp.concatenate([kernel_rows, cot_rows], axis=2), "grp").reshape(128, 3584)
+    core = (lax.axis_index("gz") & 1).astype(jnp.int32).reshape(1)
+    (halves,) = call(
+        spread_half,
+        "spread_half",
+        [((group, 8, HALF + 128), BF16)],
+        coarse_kernel.T, jnp.swapaxes(cotangent[:, 0], 1, 2),
+        core=core,
+        moved=False,
+    )
+    mine = exchange(halves, "grp").reshape(128, HALF + 128)
     ahead, behind = call(
         place_weights,
         "place_weights",
         [((9, 128, 256), BF16), ((9, 256, 128), BF16)],
         fine_kernel.T,
+        far=(1,),
     )
 
     coarse_in, slope, windows, pooled = call(
@@ -303,40 +348,47 @@
         [((64, 128), BF16), ((256, 128), F32), ((4, 128, 256), BF16), ((64, 512), BF16)],
         vol, before, after, ahead, down_kernel,
         scratch=[((256, 128), F32)],
+        far=(2,),
     )
     in_before, in_after = from_sides(coarse_in, coarse_in)
-    coarse_grad, features = call(
+    mine, in_before, in_after = lax.optimization_barrier((mine, in_before, in_after))
+    other = lax.ppermute(mine, "gz", [(i, i ^ 1) for i in range(slabs)])
+    coarse_grad, features, packed = call(
         coarse_forward,
         "coarse_forward",
-        [((64, 128), BF16), ((128, 128), BF16)],
-        coarse_in, in_before, in_after, packed,
+        [((64, 128), BF16), ((128, 128), BF16), ((128, 3456), BF16)],
+        coarse_in, in_before, in_after, mine, other,
         scratch=[((128, 128), F32)],
+        core=core,
     )
     grad_before, grad_after = from_sides(coarse_grad, coarse_grad)
-    (parts,) = call(
-        assemble,
-        "assemble",
-        [((group, 80, 128), BF16)],
-        coarse_in, features, grad_before, grad_after,
-    )
-    parts = exchange(parts, "grp")
-    shared, fine_grad = call(
+    parts, fine_grad = call(
         backward,
         "backward",
-        [((1536, 128), BF16), ((2, 128, 128), BF16)],
+        [((group, 176, 128), BF16), ((2, 128, 128), BF16)],
         coarse_grad, grad_before, grad_after, packed, pooled, slope, windows, down_kernel,
-        scratch=[((256, 128), F32)],
-    )
-    shared = exchange(shared.reshape(slabs, 48, 128), "gz")
+        coarse_in, features,
+        scratch=[((256, 128), F32), ((1536, 128), BF16)],
+    )
+    parts = exchange(parts, "grp")
     out_rows, terms = call(
         coarse_kernel_terms,
         "coarse_kernel_terms",
-        [((group, 8, 64), BF16), ((slabs, 8, 128), BF16)],
+        [((group, 8, 64), BF16), ((slabs, 16, 128), BF16)],
         parts,
         scratch=[((72, 1024), F32), ((1024, 384), BF16)],
-        final=1,
+        far=(0,),
     )
     terms = exchange(terms, "gz")
+    (terms,) = call(sum_slabs, "sum_slabs", [((slabs, 16, 128), BF16)], terms)
+    terms = exchange(terms, "gz")
+    coarse_kg, shared = call(
+        collect, "collect", [((8, 3456), F32), ((group, 96, 128), BF16)], terms, far=(0,)
+    )
+    shared = exchange(shared, "grp").reshape(1536, 128)
+    fine_kg, down_kg = call(
+        unpack, "unpack", [((64, 1728), F32), ((512, 128), F32)], shared, far=(0, 1)
+    )
     fine_before, fine_after = from_sides(fine_grad[1], fine_grad[0])
     (volume_grad,) = call(
         fine_backward,
@@ -344,18 +396,7 @@
         [((2, 16, 1024), BF16)],
         fine_grad, fine_before, fine_after, behind,
         scratch=[((4, 128, 256), BF16)],
-        final=1,
-    )
-    (shared,) = call(sum_slabs, "sum_slabs", [((group, 48, 128), BF16)], shared)
-    shared = exchange(shared, "grp")
-    (final,) = call(sum_groups, "sum_groups", [((slabs, 56, 128), BF16)], shared, terms)
-    final = exchange(final, "gz")
-    fine_kg, down_kg, coarse_kg = call(
-        unpack,
-        "unpack",
-        [((64, 1728), F32), ((512, 128), F32), ((8, 3456), F32)],
-        final,
-        final=3,
+        far=(0,),
     )
     coarse_out = jnp.swapaxes(out_rows, 1, 2)[:, None]
     return (coarse_out, volume_grad[None], fine_kg.T, down_kg, coarse_kg.T)

time: 145 us -> 133 us (0.917)
  blocking collectives: 14 us -> 67.2 us
  waiting for transfers between devices: 52.7 us -> 13.5 us
  starting transfers between devices: 63.6 us -> 41.4 us
  local copies, waits for them, and re-layouts: 3.62 us -> 0.03 us
    all_to_all x1 -> x3, blocking collectives: 14 us -> 67.2 us  [exchange(): return lax.all_to_all(blocks, axis, 0, 0, tiled=True)]
    all_to_all x5 -> x2, waiting for transfers between devices: 49.6 us -> 9.33 us  [exchange(): return lax.all_to_all(blocks, axis, 0, 0, tiled=True)]
    all_to_all x5 -> x2, starting transfers between devices: 39 us -> 14 us  [exchange(): return lax.all_to_all(blocks, axis, 0, 0, tiled=True)]
    ppermute x0 -> x1, starting transfers between devices: none -> 4.42 us  [per_device(): other = lax.ppermute(mine, 'gz', [(i, i ^ 1) for i in range(slabs)])]
    unnamed x16 -> x10, local copies, waits for them, and re-layouts: 2.73 us -> 0.02 us
    ppermute x8, starting transfers between devices: 24.6 us -> 23 us  [from_sides(): return (lax.ppermute(last, 'gz', up), lax.ppermute(first, 'gz', down))]
    ppermute x0 -> x1, waiting for transfers between devices: none -> 1.47 us  [per_device(): other = lax.ppermute(mine, 'gz', [(i, i ^ 1) for i in range(slabs)])]
  transfers between devices with their start and end apart: 13 -> 11, of which waited for: 9 -> 7; matrix products, arithmetic and copies ran while one was open for 0% -> 0% of each run, Pallas kernels for 3% -> 2%
where the time goes in v4:
time: 133 us; the launch traced here: 132 us
  blocking collectives  67.2 us (51%)
  starting transfers between devices  41.4 us (31%)
  waiting for transfers between devices  13.5 us (10%)
  Pallas kernels  8.97 us (7%)
    all_to_all x3, blocking collectives, exchange(): return lax.all_to_all(blocks, axis, 0, 0, tiled=True)  67.2 us
    ppermute x8, starting transfers between devices, from_sides(): return (lax.ppermute(last, 'gz', up), lax.ppermute(first, 'gz', down))  23 us
    all_to_all x2, starting transfers between devices, exchange(): return lax.all_to_all(blocks, axis, 0, 0, tiled=True)  14 us
    all_to_all x2, waiting for transfers between devices, exchange(): return lax.all_to_all(blocks, axis, 0, 0, tiled=True)  9.33 us
    pallas_call x10, Pallas kernels, call(): pl.pallas_call(body, out_shape=[put(*out) for put, out in zip(place, outs...  8.97 us
    ppermute x1, starting transfers between devices, per_device(): other = lax.ppermute(mine, 'gz', [(i, i ^ 1) for i in range(slabs)])  4.42 us
    ppermute x8, waiting for transfers between devices, from_sides(): return (lax.ppermute(last, 'gz', up), lax.ppermute(first, 'gz', down))  2.69 us
  transfers between devices with their start and end apart: 11, of which 7 were waited for; matrix products, arithmetic and copies ran while one was open for 0% of the time, Pallas kernels for 2%

profile of v4, /device:TPU:1, one launch (start us, length us, event | category | flops | bytes accessed | tf_op | source)
XLA Modules:
  0.0 131.9 jit_solution(3340445094522577536)
XLA Ops:
  0.6 1.7 %spread_half.1 = bf16[16,8,1920]{2,1,0:T(8,128)(2,1)} custom-call(s32[1]{0:T(128)} %bitcast.core, bf16[8,3456]{1,0:T(8,128)(2,1)} %bitcast.30, bf16[16,8,64]{2,1,0:T(8,128)(2,1)} %bitcast.31), custom_call_target="tpu_custom_call" | custom-call | flops 250000000 | bytes 1048576 | tf_op jit(solution)/shard_map/spread_half/pallas_call | solution.py:296
  2.3 10.3 %all-to-all-start = ((bf16[16,8,1920]{2,1,0:T(8,128)(2,1)}), bf16[16,8,1920]{2,1,0:T(8,128)(2,1)S(1)}, u32[]{:S(2)}, u32[]{:S(2)}) async-start(bf16[16,8,1920]{2,1,0:T(8,128)(2,1)} %spread_half.1), calls=%async_computation | async-start | bytes 983040 | tf_op jit(solution)/shard_map/all_to_all | solution.py:319
  12.7 2.9 %collective-permute-start.1 = (bf16[16,1024]{1,0:T(8,128)(2,1)S(1)}, bf16[16,1024]{1,0:T(8,128)(2,1)S(1)}, u32[]{:S(2)}, u32[]{:S(2)}) collective-permute-start(bf16[16,1024]{1,0:T(8,128)(2,1)S(1)} %get-tuple-element.52), channel_id=1, source_target_pairs={{16,0},{32,16},{48,32},{64,48},{80,64},{96,80},{112,96},{128,112},... | collective-permute-start | bytes 98312 | tf_op jit(solution)/shard_map/ppermute | solution.py:315
  15.5 2.7 %collective-permute-start = (bf16[16,1024]{1,0:T(8,128)(2,1)S(1)}, bf16[16,1024]{1,0:T(8,128)(2,1)S(1)}, u32[]{:S(2)}, u32[]{:S(2)}) collective-permute-start(bf16[16,1024]{1,0:T(8,128)(2,1)S(1)} %get-tuple-element.53), channel_id=1, source_target_pairs={{0,16},{16,32},{32,48},{48,64},{64,80},{80,96},{96,112},{112,128},... | collective-permute-start | bytes 98312 | tf_op jit(solution)/shard_map/ppermute | solution.py:315
  18.3 0.0 copy-start.1
  18.3 1.0 place_weights.1
  19.3 0.0 collective-permute-done.1.after
  19.3 0.8 fine_forward.1
  20.1 1.9 %collective-permute-start.3 = (bf16[64,128]{1,0:T(8,128)(2,1)S(1)}, bf16[64,128]{1,0:T(8,128)(2,1)S(1)}, u32[]{:S(2)}, u32[]{:S(2)}) collective-permute-start(bf16[64,128]{1,0:T(8,128)(2,1)S(1)} %get-tuple-element.26.own.coarse_in), channel_id=1, source_target_pairs={{16,0},{32,16},{48,32},{64,48},{80,64},{96,80},{112,96},{128,112},... | collective-permute-start | bytes 49160 | tf_op jit(solution)/shard_map/ppermute | solution.py:315
  22.0 4.4 %collective-permute-start.2 = (bf16[64,128]{1,0:T(8,128)(2,1)S(1)}, bf16[64,128]{1,0:T(8,128)(2,1)S(1)}, u32[]{:S(2)}, u32[]{:S(2)}) collective-permute-start(bf16[64,128]{1,0:T(8,128)(2,1)S(1)} %get-tuple-element.26.own.coarse_in), channel_id=1, source_target_pairs={{0,16},{16,32},{32,48},{48,64},{64,80},{80,96},{96,112},{112,128},... | collective-permute-start | bytes 49160 | tf_op jit(solution)/shard_map/ppermute | solution.py:315
  26.4 0.2 collective-permute-done.3.after
  26.6 0.7 collective-permute-done.2.before
  27.3 1.9 %all-to-all-done = bf16[16,8,1920]{2,1,0:T(8,128)(2,1)S(1)} async-done(((bf16[16,8,1920]{2,1,0:T(8,128)(2,1)}), bf16[16,8,1920]{2,1,0:T(8,128)(2,1)S(1)}, u32[]{:S(2)}, u32[]{:S(2)}) %all-to-all-start) | async-done | bytes 491552 | tf_op jit(solution)/shard_map/all_to_all | solution.py:319
  29.2 4.4 %collective-permute-start.4 = (bf16[128,1920]{1,0:T(8,128)(2,1)S(1)}, bf16[128,1920]{1,0:T(8,128)(2,1)S(1)}, u32[]{:S(2)}, u32[]{:S(2)}) collective-permute-start(bf16[128,1920]{1,0:T(8,128)(2,1)S(1)} %bitcast.25), channel_id=1, source_target_pairs={{0,16},{16,0},{32,48},{48,32},{64,80},{80,64},{96,112},{112,96},{1... | collective-permute-start | bytes 1474568 | tf_op jit(solution)/shard_map/ppermute | solution.py:355
  33.7 1.5 %collective-permute-done.4.other = bf16[128,1920]{1,0:T(8,128)(2,1)S(1)} collective-permute-done((bf16[128,1920]{1,0:T(8,128)(2,1)S(1)}, bf16[128,1920]{1,0:T(8,128)(2,1)S(1)}, u32[]{:S(2)}, u32[]{:S(2)}) %collective-permute-start.4) | collective-permute-done | bytes 491552 | tf_op jit(solution)/shard_map/ppermute | solution.py:355
  35.1 0.7 coarse_forward.1
  35.8 2.3 %collective-permute-start.6 = (bf16[64,128]{1,0:T(8,128)(2,1)S(1)}, bf16[64,128]{1,0:T(8,128)(2,1)S(1)}, u32[]{:S(2)}, u32[]{:S(2)}) collective-permute-start(bf16[64,128]{1,0:T(8,128)(2,1)S(1)} %get-tuple-element.30.own), channel_id=1, source_target_pairs={{16,0},{32,16},{48,32},{64,48},{80,64},{96,80},{112,96},{128,112},... | collective-permute-start | bytes 49160 | tf_op jit(solution)/shard_map/ppermute | solution.py:315
  38.1 3.3 %collective-permute-start.5 = (bf16[64,128]{1,0:T(8,128)(2,1)S(1)}, bf16[64,128]{1,0:T(8,128)(2,1)S(1)}, u32[]{:S(2)}, u32[]{:S(2)}) collective-permute-start(bf16[64,128]{1,0:T(8,128)(2,1)S(1)} %get-tuple-element.30.own), channel_id=1, source_target_pairs={{0,16},{16,32},{32,48},{48,64},{64,80},{80,96},{96,112},{112,128},... | collective-permute-start | bytes 49160 | tf_op jit(solution)/shard_map/ppermute | solution.py:315
  41.4 0.8 collective-permute-done.5.before
  42.3 1.0 backward.1
  43.2 29.4 %all_to_all.25.parts = bf16[16,176,128]{2,1,0:T(8,128)(2,1)S(1)} all-to-all(bf16[16,176,128]{2,1,0:T(8,128)(2,1)S(1)} %get-tuple-element.36), channel_id=1, replica_groups=mesh['gz'=32,'grp'=16] {'grp'}, dimensions={0} | all-to-all | bytes 1441792 | tf_op jit(solution)/shard_map/all_to_all | solution.py:319
  72.6 0.9 coarse_kernel_terms.1
  73.5 25.3 %all_to_all.26.terms = bf16[32,16,128]{2,1,0:T(8,128)(2,1)S(1)} all-to-all(bf16[32,16,128]{2,1,0:T(8,128)(2,1)S(1)} %get-tuple-element.40), channel_id=1, replica_groups=mesh['gz'=32,'grp'=16] {'gz'}, dimensions={0} | all-to-all | bytes 262144 | tf_op jit(solution)/shard_map/all_to_all | solution.py:319
  98.9 12.5 %all_to_all.27.terms = bf16[32,16,128]{2,1,0:T(8,128)(2,1)S(1)} all-to-all(bf16[32,16,128]{2,1,0:T(8,128)(2,1)S(1)} %sum_slabs.1), channel_id=1, replica_groups=mesh['gz'=32,'grp'=16] {'gz'}, dimensions={0} | all-to-all | bytes 262144 | tf_op jit(solution)/shard_map/all_to_all | solution.py:319
  111.4 0.8 collect.1
  112.2 3.7 %all-to-all-start.4 = ((bf16[16,96,128]{2,1,0:T(8,128)(2,1)}), bf16[16,96,128]{2,1,0:T(8,128)(2,1)S(1)}, u32[]{:S(2)}, u32[]{:S(2)}) async-start(bf16[16,96,128]{2,1,0:T(8,128)(2,1)} %get-tuple-element.41), calls=%async_computation.4 | async-start | bytes 786432 | tf_op jit(solution)/shard_map/all_to_all | solution.py:319
  116.0 2.4 %collective-permute-start.8 = (bf16[128,128]{1,0:T(8,128)(2,1)S(1)}, bf16[128,128]{1,0:T(8,128)(2,1)S(1)}, u32[]{:S(2)}, u32[]{:S(2)}) collective-permute-start(bf16[128,128]{1,0:T(8,128)(2,1)S(1)} %get-tuple-element.50), channel_id=1, source_target_pairs={{16,0},{32,16},{48,32},{64,48},{80,64},{96,80},{112,96},{128,112},... | collective-permute-start | bytes 98312 | tf_op jit(solution)/shard_map/ppermute | solution.py:315
  118.3 3.2 %collective-permute-start.7 = (bf16[128,128]{1,0:T(8,128)(2,1)S(1)}, bf16[128,128]{1,0:T(8,128)(2,1)S(1)}, u32[]{:S(2)}, u32[]{:S(2)}) collective-permute-start(bf16[128,128]{1,0:T(8,128)(2,1)S(1)} %get-tuple-element.51), channel_id=1, source_target_pairs={{0,16},{16,32},{32,48},{48,64},{64,80},{80,96},{96,112},{112,128},... | collective-permute-start | bytes 98312 | tf_op jit(solution)/shard_map/ppermute | solution.py:315
  121.5 1.0 collective-permute-done.7.before
  122.5 1.1 fine_backward.1
  123.7 7.4 %all-to-all-done.4 = bf16[16,96,128]{2,1,0:T(8,128)(2,1)S(1)} async-done(((bf16[16,96,128]{2,1,0:T(8,128)(2,1)}), bf16[16,96,128]{2,1,0:T(8,128)(2,1)S(1)}, u32[]{:S(2)}, u32[]{:S(2)}) %all-to-all-start.4) | async-done | bytes 393248 | tf_op jit(solution)/shard_map/all_to_all | solution.py:319
  131.0 0.9 unpack.1
  (15 shorter events, 0.1 us)
Async XLA Ops:
  2.3 10.3 %copy-start.2 = (bf16[1,2,16,1024]{3,2,1,0:T(8,128)(2,1)S(1)}, bf16[1,2,16,1024]{3,2,1,0:T(8,128)(2,1)}, u32[]{:S(2)}) copy-start(bf16[1,2,16,1024]{3,2,1,0:T(8,128)(2,1)} %param.5) | copy-start | bytes 196612
  2.3 15.9 %copy-start.3 = (bf16[1728,64]{0,1:T(8,128)(2,1)S(1)}, bf16[1728,64]{0,1:T(8,128)(2,1)}, u32[]{:S(2)}) copy-start(bf16[1728,64]{0,1:T(8,128)(2,1)} %param.7) | copy-start | bytes 663556
  2.3 26.9 %all-to-all-start = ((bf16[16,8,1920]{2,1,0:T(8,128)(2,1)}), bf16[16,8,1920]{2,1,0:T(8,128)(2,1)S(1)}, u32[]{:S(2)}, u32[]{:S(2)}) async-start(bf16[16,8,1920]{2,1,0:T(8,128)(2,1)} %spread_half.1), calls=%async_computation | async-start | bytes 983040 | tf_op jit(solution)/shard_map/all_to_all | solution.py:319
  12.7 6.6 %collective-permute-start.1 = (bf16[16,1024]{1,0:T(8,128)(2,1)S(1)}, bf16[16,1024]{1,0:T(8,128)(2,1)S(1)}, u32[]{:S(2)}, u32[]{:S(2)}) collective-permute-start(bf16[16,1024]{1,0:T(8,128)(2,1)S(1)} %get-tuple-element.52), channel_id=1, source_target_pairs={{16,0},{32,16},{48,32},{64,48},{80,64},{96,80},{112,96},{128,112},... | collective-permute-start | bytes 98312 | tf_op jit(solution)/shard_map/ppermute | solution.py:315
  15.5 3.7 %collective-permute-start = (bf16[16,1024]{1,0:T(8,128)(2,1)S(1)}, bf16[16,1024]{1,0:T(8,128)(2,1)S(1)}, u32[]{:S(2)}, u32[]{:S(2)}) collective-permute-start(bf16[16,1024]{1,0:T(8,128)(2,1)S(1)} %get-tuple-element.53), channel_id=1, source_target_pairs={{0,16},{16,32},{32,48},{48,64},{64,80},{80,96},{96,112},{112,128},... | collective-permute-start | bytes 98312 | tf_op jit(solution)/shard_map/ppermute | solution.py:315
  18.3 1.0 copy-start.1
  20.1 6.5 %collective-permute-start.3 = (bf16[64,128]{1,0:T(8,128)(2,1)S(1)}, bf16[64,128]{1,0:T(8,128)(2,1)S(1)}, u32[]{:S(2)}, u32[]{:S(2)}) collective-permute-start(bf16[64,128]{1,0:T(8,128)(2,1)S(1)} %get-tuple-element.26.own.coarse_in), channel_id=1, source_target_pairs={{16,0},{32,16},{48,32},{64,48},{80,64},{96,80},{112,96},{128,112},... | collective-permute-start | bytes 49160 | tf_op jit(solution)/shard_map/ppermute | solution.py:315
  22.0 5.3 %collective-permute-start.2 = (bf16[64,128]{1,0:T(8,128)(2,1)S(1)}, bf16[64,128]{1,0:T(8,128)(2,1)S(1)}, u32[]{:S(2)}, u32[]{:S(2)}) collective-permute-start(bf16[64,128]{1,0:T(8,128)(2,1)S(1)} %get-tuple-element.26.own.coarse_in), channel_id=1, source_target_pairs={{0,16},{16,32},{32,48},{48,64},{64,80},{80,96},{96,112},{112,128},... | collective-permute-start | bytes 49160 | tf_op jit(solution)/shard_map/ppermute | solution.py:315
  29.2 13.0 %copy-start = (bf16[4,128,256]{2,1,0:T(8,128)(2,1)S(1)}, bf16[4,128,256]{2,1,0:T(8,128)(2,1)}, u32[]{:S(2)}) copy-start(bf16[4,128,256]{2,1,0:T(8,128)(2,1)} %get-tuple-element.34.windows) | copy-start | bytes 786436
  29.2 5.9 %collective-permute-start.4 = (bf16[128,1920]{1,0:T(8,128)(2,1)S(1)}, bf16[128,1920]{1,0:T(8,128)(2,1)S(1)}, u32[]{:S(2)}, u32[]{:S(2)}) collective-permute-start(bf16[128,1920]{1,0:T(8,128)(2,1)S(1)} %bitcast.25), channel_id=1, source_target_pairs={{0,16},{16,0},{32,48},{48,32},{64,80},{80,64},{96,112},{112,96},{1... | collective-permute-start | bytes 1474568 | tf_op jit(solution)/shard_map/ppermute | solution.py:355
  35.8 5.6 %collective-permute-start.6 = (bf16[64,128]{1,0:T(8,128)(2,1)S(1)}, bf16[64,128]{1,0:T(8,128)(2,1)S(1)}, u32[]{:S(2)}, u32[]{:S(2)}) collective-permute-start(bf16[64,128]{1,0:T(8,128)(2,1)S(1)} %get-tuple-element.30.own), channel_id=1, source_target_pairs={{16,0},{32,16},{48,32},{64,48},{80,64},{96,80},{112,96},{128,112},... | collective-permute-start | bytes 49160 | tf_op jit(solution)/shard_map/ppermute | solution.py:315
  38.1 4.1 %collective-permute-start.5 = (bf16[64,128]{1,0:T(8,128)(2,1)S(1)}, bf16[64,128]{1,0:T(8,128)(2,1)S(1)}, u32[]{:S(2)}, u32[]{:S(2)}) collective-permute-start(bf16[64,128]{1,0:T(8,128)(2,1)S(1)} %get-tuple-element.30.own), channel_id=1, source_target_pairs={{0,16},{16,32},{32,48},{48,64},{64,80},{80,96},{96,112},{112,128},... | collective-permute-start | bytes 49160 | tf_op jit(solution)/shard_map/ppermute | solution.py:315
  112.2 10.3 %copy-start.4 = (bf16[9,256,128]{2,1,0:T(8,128)(2,1)S(1)}, bf16[9,256,128]{2,1,0:T(8,128)(2,1)}, u32[]{:S(2)}) copy-start(bf16[9,256,128]{2,1,0:T(8,128)(2,1)} %get-tuple-element.39.weights) | copy-start | bytes 1769476
  112.2 18.8 %all-to-all-start.4 = ((bf16[16,96,128]{2,1,0:T(8,128)(2,1)}), bf16[16,96,128]{2,1,0:T(8,128)(2,1)S(1)}, u32[]{:S(2)}, u32[]{:S(2)}) async-start(bf16[16,96,128]{2,1,0:T(8,128)(2,1)} %get-tuple-element.41), calls=%async_computation.4 | async-start | bytes 786432 | tf_op jit(solution)/shard_map/all_to_all | solution.py:319
  116.0 5.6 %collective-permute-start.8 = (bf16[128,128]{1,0:T(8,128)(2,1)S(1)}, bf16[128,128]{1,0:T(8,128)(2,1)S(1)}, u32[]{:S(2)}, u32[]{:S(2)}) collective-permute-start(bf16[128,128]{1,0:T(8,128)(2,1)S(1)} %get-tuple-element.50), channel_id=1, source_target_pairs={{16,0},{32,16},{48,32},{64,48},{80,64},{96,80},{112,96},{128,112},... | collective-permute-start | bytes 98312 | tf_op jit(solution)/shard_map/ppermute | solution.py:315
  118.3 4.2 %collective-permute-start.7 = (bf16[128,128]{1,0:T(8,128)(2,1)S(1)}, bf16[128,128]{1,0:T(8,128)(2,1)S(1)}, u32[]{:S(2)}, u32[]{:S(2)}) collective-permute-start(bf16[128,128]{1,0:T(8,128)(2,1)S(1)} %get-tuple-element.51), channel_id=1, source_target_pairs={{0,16},{16,32},{32,48},{48,64},{64,80},{80,96},{96,112},{112,128},... | collective-permute-start | bytes 98312 | tf_op jit(solution)/shard_map/ppermute | solution.py:315
